TPU v7x, 256 devices: a whole 4x4x8 slice. The times are simulated.
256 devices in a mesh: grid: 64 (over z, x, core), band: 4 (over y).
Axes of the slice: x: 4, y: 4, z: 8, core: 2. Of those that a mesh axis runs over, the one named last changes fastest.
Arguments:
- basis: float32 [2048, 65536], P('band', 'grid'), as said below
- panel: float32 [1024, 65536], P('band', 'grid'), may hold values from -6 to 6
Outputs:
- new_panel: float32 [1024, 65536], P('band', 'grid')
- coeffs: float32 [2048, 1024], P('band')
Inputs may be any that keep to these rules, and one draw needn't show every extreme that they name: The rows of basis are orthogonal to each other, each with squared sum 65536 (to float32 rounding).
All inputs are finite; a program needn't handle non-finite values.
Results may differ from a plain program's by a relative error of at most 0.000073.
Values sent between devices are 32-bit elements; how exact they have to be, the bound alone decides.
A program may use at most 128 MiB of HBM per device.

v0:
```python
import jax
import jax.numpy as jnp
from jax import lax
from jax.sharding import PartitionSpec as P


def together(arrays, axis):
    ravelled, at, finished = (jnp.concatenate([a.reshape(-1) for a in arrays]), 0, [])
    total = lax.psum(ravelled, axis)
    for a in arrays:
        finished.append(total[at : at + a.size].reshape(a.shape))
        at += a.size
    return tuple(finished)


def cut_along(array, dim, count):
    before, after = (array.shape[:dim], array.shape[dim + 1 :])
    return jnp.moveaxis(array.reshape(*before, count, -1, *after), dim, 0)


def summed_on_arrival(array, axis, dim):
    blocks = cut_along(array, dim, lax.axis_size(axis))
    arrived = lax.all_to_all(blocks, axis, split_axis=0, concat_axis=0, tiled=True)
    return arrived.sum(axis=0)


def tdot(left, right):
    return lax.dot_general(
        left,
        right,
        (((1,), (1,)), ((), ())),
        precision=lax.Precision.HIGHEST,
        preferred_element_type=jnp.float32,
    )


def ndot(left, right):
    return jnp.dot(left, right, precision=lax.Precision.HIGHEST)


def body(basis, panel):
    n_grid = panel.shape[1] * lax.axis_size("grid")
    n_band = lax.axis_size("band")
    rows_q = basis.shape[0]
    rows_p = panel.shape[0]
    n_panel = rows_p * n_band
    stacked = jnp.concatenate([basis, panel], 0)
    both = tdot(stacked, lax.all_gather(panel, "band", axis=0, tiled=True))
    coeff_sum, gram_sum = together((both[:rows_q], both[rows_q:]), "grid")
    coeffs = coeff_sum / n_grid
    projected = panel - lax.psum_scatter(
        ndot(coeffs.T, basis), "band", scatter_dimension=0, tiled=True
    )
    gram_part = gram_sum / n_grid - summed_on_arrival(ndot(coeffs.T, coeffs), "band", 0)
    gram = lax.all_gather(gram_part, "band", axis=0, tiled=True)
    factor = jnp.linalg.cholesky(gram)
    offset = lax.axis_index("band") * rows_p
    row_ids = lax.broadcasted_iota(jnp.int32, (n_panel, rows_p), 0)
    col_ids = lax.broadcasted_iota(jnp.int32, (n_panel, rows_p), 1)
    unit_cols = (row_ids == col_ids + offset).astype(jnp.float32)
    inverse_rows = lax.linalg.triangular_solve(
        factor, unit_cols, left_side=True, lower=True, transpose_a=True
    ).T
    new_panel = ndot(inverse_rows, lax.all_gather(projected, "band", axis=0, tiled=True))
    return (new_panel, coeffs)


def solution(mesh):
    placed = (P("band", "grid"), P("band", "grid"))
    return jax.shard_map(
        body,
        mesh=mesh,
        in_specs=placed,
        out_specs=(P("band", "grid"), P("band", None)),
        check_vma=False,
    )
```

profile of v0, /device:TPU:1, one launch (start us, length us, event | category | flops | bytes accessed | tf_op | source)
XLA Modules:
  0.0 784.5 jit_solution(712397003574629770)
XLA Ops:
  7.9 56.3 %all-gather.4.cloned.1.call-done = f32[1024,1024]{1,0:T(8,128)} async-done(((f32[256,1024]{1,0:T(8,128)}), f32[1024,1024]{1,0:T(8,128)}) %all-gather.4.cloned.1.call-update) | async-done | bytes 4194320 | tf_op jit(solution)/shard_map/all_gather | solution.py:48
  64.2 12.5 %fusion.1 = f32[768,1024]{1,0:T(8,128)S(1)} fusion(f32[1024,1024]{1,0:T(8,128)} %all-gather.4.cloned.1.call-done, f32[256,1024]{1,0:T(8,128)} %param.3, f32[512,1024]{1,0:T(8,128)} %param.2), kind=kOutput, calls=%fused_computation.6 | convolution fusion | flops 9664462848 | bytes 10485760 | tf_op jit(solution)/shard_map/dot_general | solution.py:28
  80.0 192.0 %all-reduce.3.cloned.1.call-done = f32[786432]{0:T(1024)} async-done(((f32[786432]{0:T(1024)}), f32[786432]{0:T(1024)}) %all-reduce.3.cloned.1.call-update) | async-done | bytes 3145744 | tf_op jit(solution)/shard_map/psum | solution.py:9
  275.3 10.2 %fusion.69 = f32[1024,1024]{1,0:T(8,128)} fusion(f32[512,1024]{1,0:T(8,128)} %div.29, f32[512,1024]{1,0:T(8,128)} %param.2), kind=kOutput, calls=%fused_computation.169 | convolution fusion | flops 6442450944 | bytes 8388608 | tf_op jit(solution)/shard_map/dot_general | solution.py:38
  290.1 9.9 %fusion.68 = f32[4,256,1024]{2,1,0:T(8,128)} fusion(f32[4,256,512]{2,1,0:T(8,128)} %bitcast.110, f32[512,1024,1]{1,0,2:T(8,128)S(1)} %copy-done.2), kind=kOutput, calls=%fused_computation.168 | convolution fusion | flops 6442450944 | bytes 8388608 | tf_op jit(solution)/shard_map/dot_general | solution.py:38
  306.7 72.1 %all-to-all-done = f32[4,256,1024]{2,1,0:T(8,128)} async-done(((f32[4,256,1024]{2,1,0:T(8,128)}), f32[4,256,1024]{2,1,0:T(8,128)}, u32[]{:S(2)}, u32[]{:S(2)}) %all-to-all-start) | async-done | bytes 4194336 | tf_op jit(solution)/shard_map/all_to_all | solution.py:23
  388.1 48.0 %all-gather.6.cloned.1.call-done = f32[1024,1024]{0,1:T(8,128)} async-done(((f32[256,1024]{0,1:T(8,128)}), f32[1024,1024]{0,1:T(8,128)}) %all-gather.6.cloned.1.call-update) | async-done | bytes 4194320 | tf_op jit(solution)/shard_map/all_gather | solution.py:55
  448.0 11.7 %cholesky.223 = f32[128,128]{1,0:T(8,128)S(1)} custom-call(f32[128,128]{1,0:T(8,128)S(1)} %cholesky.580), custom_call_target="Cholesky" | custom-call | tf_op jit(solution)/shard_map/jit(cholesky)/cholesky | solution.py:56
  462.2 9.8 %custom-call.62 = f32[1,128,128]{1,2,0:T(8,128)S(1)} custom-call(f32[1,128,128]{2,1,0:T(8,128)S(1)} %get-tuple-element.41), custom_call_target="InvertDiagBlocksLowerTriangular" | custom-call | tf_op jit(solution)/shard_map/jit(cholesky)/cholesky | solution.py:56
  476.0 11.9 %cholesky.244 = f32[128,128]{1,0:T(8,128)S(1)} custom-call(f32[128,128]{1,0:T(8,128)S(1)} %cholesky.584), custom_call_target="Cholesky" | custom-call | tf_op jit(solution)/shard_map/jit(cholesky)/cholesky | solution.py:56
  488.5 9.8 %custom-call.63 = f32[1,128,128]{1,2,0:T(8,128)S(1)} custom-call(f32[1,128,128]{2,1,0:T(8,128)S(1)} %get-tuple-element.38), custom_call_target="InvertDiagBlocksLowerTriangular" | custom-call | tf_op jit(solution)/shard_map/jit(cholesky)/cholesky | solution.py:56
  501.7 11.7 %cholesky.468 = f32[128,128]{1,0:T(8,128)S(1)} custom-call(f32[128,128]{1,0:T(8,128)S(1)} %cholesky.589), custom_call_target="Cholesky" | custom-call | tf_op jit(solution)/shard_map/jit(cholesky)/cholesky | solution.py:56
  514.7 9.8 %custom-call.64 = f32[1,128,128]{1,2,0:T(8,128)S(1)} custom-call(f32[1,128,128]{2,1,0:T(8,128)S(1)} %get-tuple-element.35), custom_call_target="InvertDiagBlocksLowerTriangular" | custom-call | tf_op jit(solution)/shard_map/jit(cholesky)/cholesky | solution.py:56
  528.0 12.1 %cholesky.487 = f32[128,128]{1,0:T(8,128)S(1)} custom-call(f32[128,128]{1,0:T(8,128)S(1)} %cholesky.594), custom_call_target="Cholesky" | custom-call | tf_op jit(solution)/shard_map/jit(cholesky)/cholesky | solution.py:56
  541.4 9.8 %custom-call.65 = f32[1,128,128]{1,2,0:T(8,128)S(1)} custom-call(f32[1,128,128]{2,1,0:T(8,128)S(1)} %get-tuple-element.32), custom_call_target="InvertDiagBlocksLowerTriangular" | custom-call | tf_op jit(solution)/shard_map/jit(cholesky)/cholesky | solution.py:56
  554.7 11.7 %cholesky.506 = f32[128,128]{1,0:T(8,128)S(1)} custom-call(f32[128,128]{1,0:T(8,128)S(1)} %cholesky.599), custom_call_target="Cholesky" | custom-call | tf_op jit(solution)/shard_map/jit(cholesky)/cholesky | solution.py:56
  567.7 9.9 %custom-call.66 = f32[1,128,128]{1,2,0:T(8,128)S(1)} custom-call(f32[1,128,128]{2,1,0:T(8,128)S(1)} %get-tuple-element.29), custom_call_target="InvertDiagBlocksLowerTriangular" | custom-call | tf_op jit(solution)/shard_map/jit(cholesky)/cholesky | solution.py:56
  581.0 11.7 %cholesky.526 = f32[128,128]{1,0:T(8,128)S(1)} custom-call(f32[128,128]{1,0:T(8,128)S(1)} %cholesky.604), custom_call_target="Cholesky" | custom-call | tf_op jit(solution)/shard_map/jit(cholesky)/cholesky | solution.py:56
  593.9 9.8 %custom-call.67 = f32[1,128,128]{1,2,0:T(8,128)S(1)} custom-call(f32[1,128,128]{2,1,0:T(8,128)S(1)} %get-tuple-element.26), custom_call_target="InvertDiagBlocksLowerTriangular" | custom-call | tf_op jit(solution)/shard_map/jit(cholesky)/cholesky | solution.py:56
  606.7 11.9 %cholesky.546 = f32[128,128]{1,0:T(8,128)S(1)} custom-call(f32[128,128]{1,0:T(8,128)S(1)} %cholesky.609), custom_call_target="Cholesky" | custom-call | tf_op jit(solution)/shard_map/jit(cholesky)/cholesky | solution.py:56
  620.0 9.8 %custom-call.68 = f32[1,128,128]{1,2,0:T(8,128)S(1)} custom-call(f32[1,128,128]{2,1,0:T(8,128)S(1)} %get-tuple-element.23), custom_call_target="InvertDiagBlocksLowerTriangular" | custom-call | tf_op jit(solution)/shard_map/jit(cholesky)/cholesky | solution.py:56
  632.4 11.7 %cholesky.564 = f32[128,128]{1,0:T(8,128)S(1)} custom-call(f32[128,128]{1,0:T(8,128)S(1)} %convolution_subtract_fusion.13), custom_call_target="Cholesky" | custom-call | tf_op jit(solution)/shard_map/jit(cholesky)/cholesky | solution.py:56
  655.8 22.6 %while.1 = (s32[]{:T(128)}, f32[1024,1024]{1,0:T(8,128)}, s32[8,2]{0,1:T(2,128)S(1)}, f32[8,128,128]{2,1,0:T(8,128)S(1)}, s32[]{:T(128)}) while((s32[]{:T(128)}, f32[1024,1024]{1,0:T(8,128)}, s32[8,2]{0,1:T(2,128)S(1)}, f32[8,128,128]{2,1,0:T(8,128)S(1)}, s32[]{:T(128)}) %tuple.43), condition=%wide.while_cond, body=%wide.while_body.sunk | while | flops 2 | bytes 131181 | solution.py:61
  678.4 78.8 %custom-call.69 = f32[8,128,128]{1,2,0:T(8,128)S(1)} custom-call(f32[8,128,128]{2,1,0:T(8,128)S(1)} %get-tuple-element.9), custom_call_target="InvertDiagBlocksLowerTriangular" | custom-call | tf_op jit(solution)/shard_map/triangular_solve | solution.py:61
  (142 shorter events, 121.7 us)
Async XLA Ops:
  7.2 57.1 %all-gather.4.cloned.1.call-start = ((), (), s32[]{:S(2)}) async-start(), calls=%async_computation.2 | async-start | bytes 5242880 | tf_op jit(solution)/shard_map/all_gather | solution.py:48
  7.9 264.1 %all-reduce.3.cloned.1.call-start = ((), (), s32[]{:S(2)}) async-start(), calls=%async_computation.3 | async-start | bytes 6291456 | tf_op jit(solution)/shard_map/psum | solution.py:9
  79.5 306.1 %reduce-scatter.2.cloned.1.call-start = ((), (), s32[]{:S(2)}) async-start(), calls=%async_computation.5 | async-start | bytes 5242880 | tf_op jit(solution)/shard_map/reduce_scatter | solution.py:51
  287.0 3.1 copy-start.2
  299.9 78.9 %all-to-all-start = ((f32[4,256,1024]{2,1,0:T(8,128)}), f32[4,256,1024]{2,1,0:T(8,128)}, u32[]{:S(2)}, u32[]{:S(2)}) async-start(f32[4,256,1024]{2,1,0:T(8,128)} %fusion.68), calls=%async_computation | async-start | bytes 8388608 | tf_op jit(solution)/shard_map/all_to_all | solution.py:23
  304.9 131.2 %all-gather.6.cloned.1.call-start = ((), (), s32[]{:S(2)}) async-start(), calls=%async_computation.4 | async-start | bytes 5242880 | tf_op jit(solution)/shard_map/all_gather | solution.py:55
  382.5 3.1 copy-start.1
  385.3 385.5 %all-gather.8.cloned.1.call-start = ((), (), s32[]{:S(2)}) async-start(), calls=%async_computation.6 | async-start | bytes 5242880 | tf_op jit(solution)/shard_map/all_gather | solution.py:64
  446.0 2.0 copy-start
Sparse Core Ops, SparseCore 0:
  9.8 54.3 all-gather.3
  79.7 192.3 all-reduce.2
  285.6 73.5 reduce-scatter.1
  385.4 50.6 all-gather.5
  437.7 51.4 all-gather.7
where the time goes:
time: 791 us; the launch traced here: 785 us
  waiting for transfers between devices  369 us (47%)
  other arithmetic  273 us (35%)
  matrix products  75.5 us (10%)
  local copies, waits for them, and re-layouts  41.8 us (5%)
  between operations  19.7 us (2%)
    psum x1, waiting for transfers between devices, together(): total = lax.psum(ravelled, axis)  192 us
    another operation x30, other arithmetic, body(): factor = jnp.linalg.cholesky(gram)  172 us
    another operation x3, other arithmetic, body(): lax.linalg.triangular_solve(factor, unit_cols, left_side=True, lower=True...  83.7 us
    all_to_all x1, waiting for transfers between devices, summed_on_arrival(): lax.all_to_all(blocks, axis, split_axis=0, concat_axis=0, tiled=True)  72.1 us
    all_gather x1, waiting for transfers between devices, body(): both = tdot(stacked, lax.all_gather(panel, 'band', axis=0, tiled=True))  56.3 us
    all_gather x1, waiting for transfers between devices, body(): gram = lax.all_gather(gram_part, 'band', axis=0, tiled=True)  48 us
    dot_general x3, matrix products, ndot(): return jnp.dot(left, right, precision=lax.Precision.HIGHEST)  26.8 us
    another operation x14, matrix products, body(): factor = jnp.linalg.cholesky(gram)  23.1 us
  transfers between devices with their start and end apart: 6, of which 4 were waited for; matrix products, arithmetic and copies ran while one was open for 45% of the time, Pallas kernels for 0%

commit v1 on v0

--- a/solution.py
+++ b/solution.py
@@ -1,7 +1,112 @@
 import jax
 import jax.numpy as jnp
 from jax import lax
+from jax.experimental import pallas as pl
+from jax.experimental.pallas import tpu as pltpu
 from jax.sharding import PartitionSpec as P
+
+F32, BF16 = jnp.float32, jnp.bfloat16
+
+def halves(x):
+    hi = x.astype(BF16)
+    return hi, (x - hi.astype(F32)).astype(BF16)
+
+def dot3(a, b, dims):
+    (ah, al), (bh, bl) = a, b
+    dg = lambda u, v: lax.dot_general(u, v, (dims, ((), ())), preferred_element_type=F32)
+    return dg(ah, bh) + (dg(ah, bl) + dg(al, bh))
+
+NN, TN, NT = ((1,), (0,)), ((0,), (0,)), ((1,), (1,))
+BASE = 32
+
+def base_block(w, at):
+    n = w.shape[0]
+    rows = w[at:at + BASE]
+    lane = lax.broadcasted_iota(jnp.int32, (BASE, n), 1)
+    sub = lax.broadcasted_iota(jnp.int32, (BASE, n), 0)
+    cols = []
+    for j in range(BASE):
+        lo = j // 8 * 8
+        cols.append(jnp.broadcast_to(rows[lo:, at + j:at + j + 1], (BASE - lo, n)))
+    inside = (lane >= at) & (lane < at + BASE)
+    v = jnp.where(inside, (lane == sub + at).astype(F32), rows)
+    v = [v[8 * s:8 * s + 8] for s in range(BASE // 8)]
+    cols = [[c[8 * s:8 * s + 8] for s in range(c.shape[0] // 8)] for c in cols]
+    nb = BASE // 8
+    sub8 = lax.broadcasted_iota(jnp.int32, (8, n), 0)
+    bc = lambda x, i: jnp.broadcast_to(x[i:i + 1], (8, n))
+    for j in range(BASE):
+        s0, r0 = j // 8, j % 8
+        c = cols[j]
+        inv = lax.rsqrt(bc(c[0], r0))
+        l = [x * inv for x in c]
+        for jj in range(j + 1, BASE):
+            s1, r1 = jj // 8, jj % 8
+            f = bc(l[s1 - s0], r1)
+            for s in range(s1, nb):
+                cols[jj][s - s1] = cols[jj][s - s1] - l[s - s0] * f
+        piv = bc(v[s0], r0) * inv
+        l0 = jnp.where(sub8 > r0, l[0], 0.0)
+        v[s0] = jnp.where(sub8 == r0, piv, v[s0] - l0 * piv)
+        for s in range(s0 + 1, nb):
+            v[s] = v[s] - l[s - s0] * piv
+    return jnp.concatenate(v, 0)
+
+def factor128(w):
+    n = w.shape[0]
+    lane = lax.broadcasted_iota(jnp.int32, (n, n), 1)
+    row = lax.broadcasted_iota(jnp.int32, (n, n), 0)
+    for at in range(0, n, BASE):
+        v = base_block(w, at)
+        end = at + BASE
+        if end < n:
+            parts = halves(v)
+            upd = lax.dot_general(v, v, (TN, ((), ())), precision=lax.Precision.HIGHEST, preferred_element_type=F32)
+            below = w[end:]
+            l2 = lane[end:]
+            below = jnp.where((l2 >= at) & (l2 < end), 0.0, below) - upd[end:]
+            w = jnp.concatenate(([w[:at]] if at else []) + [v, below], 0)
+        else:
+            w = jnp.concatenate([w[:at], v], 0)
+    return jnp.where(lane <= row, w, 0.0)
+
+B = 128
+
+def chol_kernel(g_ref, m_ref, th, tl):
+    n = g_ref.shape[0]
+    nb = n // B
+    m_ref[...] = g_ref[...]
+
+    def step(k, _):
+        r = pl.multiple_of(k * B, B)
+        inv = factor128(m_ref[pl.ds(r, B), pl.ds(r, B)])
+        t = dot3(halves(inv), halves(m_ref[pl.ds(r, B), :]), NN)
+        m_ref[pl.ds(r, B), :] = t
+        m_ref[pl.ds(r, B), pl.ds(r, B)] = inv
+        hi, lo = halves(m_ref[pl.ds(r, B), :])
+        th[...] = hi
+        tl[...] = lo
+
+        def rest(i, _):
+            q = pl.multiple_of(i * B, B)
+            m_ref[pl.ds(q, B), pl.ds(r, B)] = jnp.zeros((B, B), F32)
+            f = (th[:, pl.ds(q, B)], tl[:, pl.ds(q, B)])
+            m_ref[pl.ds(q, B), :] = m_ref[pl.ds(q, B), :] - dot3(f, (th[...], tl[...]), TN)
+            return 0
+        lax.fori_loop(k + 1, nb, rest, 0)
+        return 0
+    lax.fori_loop(0, nb, step, 0)
+
+def inverse_factor(g):
+    n = g.shape[0]
+    return pl.pallas_call(
+        chol_kernel,
+        out_shape=jax.ShapeDtypeStruct((n, n), F32),
+        in_specs=[pl.BlockSpec(memory_space=pltpu.VMEM)],
+        out_specs=pl.BlockSpec(memory_space=pltpu.VMEM),
+        scratch_shapes=[pltpu.VMEM((B, n), BF16), pltpu.VMEM((B, n), BF16)],
+        compiler_params=pltpu.CompilerParams(vmem_limit_bytes=40 * 2**20),
+    )(g)
 
 
 def together(arrays, axis):
@@ -29,13 +134,13 @@
         left,
         right,
         (((1,), (1,)), ((), ())),
-        precision=lax.Precision.HIGHEST,
+        precision=lax.Precision.HIGH,
         preferred_element_type=jnp.float32,
     )
 
 
 def ndot(left, right):
-    return jnp.dot(left, right, precision=lax.Precision.HIGHEST)
+    return jnp.dot(left, right, precision=lax.Precision.HIGH)
 
 
 def body(basis, panel):
@@ -53,14 +158,11 @@
     )
     gram_part = gram_sum / n_grid - summed_on_arrival(ndot(coeffs.T, coeffs), "band", 0)
     gram = lax.all_gather(gram_part, "band", axis=0, tiled=True)
-    factor = jnp.linalg.cholesky(gram)
     offset = lax.axis_index("band") * rows_p
-    row_ids = lax.broadcasted_iota(jnp.int32, (n_panel, rows_p), 0)
-    col_ids = lax.broadcasted_iota(jnp.int32, (n_panel, rows_p), 1)
-    unit_cols = (row_ids == col_ids + offset).astype(jnp.float32)
-    inverse_rows = lax.linalg.triangular_solve(
-        factor, unit_cols, left_side=True, lower=True, transpose_a=True
-    ).T
+    inverse_rows = lax.dynamic_slice_in_dim(inverse_factor(gram), offset, rows_p, 0)
+    row_ids = lax.broadcasted_iota(jnp.int32, (rows_p, n_panel), 0)
+    col_ids = lax.broadcasted_iota(jnp.int32, (rows_p, n_panel), 1)
+    inverse_rows = jnp.where(col_ids <= row_ids + offset, inverse_rows, 0.0)
     new_panel = ndot(inverse_rows, lax.all_gather(projected, "band", axis=0, tiled=True))
     return (new_panel, coeffs)
 

time: 791 us -> 492 us (0.62)
  other arithmetic: 273 us -> 11.1 us
  matrix products: 75.5 us -> 28.2 us
  Pallas kernels: 0 us -> 41.5 us
  local copies, waits for them, and re-layouts: 41.8 us -> 11.4 us
  waiting for transfers between devices: 369 us -> 380 us
    another operation x33 -> x0, other arithmetic: 256 us -> none  [the longest x30 172 us: body(): factor = jnp.linalg.cholesky(gram)]
    pallas_call x0 -> x1, Pallas kernels: none -> 41.5 us  [inverse_factor(): pl.pallas_call(chol_kernel, out_shape=jax.ShapeDtypeStruct((n, n), F32),...]
    another operation x29 -> x0, matrix products: 36.1 us -> none  [the longest x14 23.1 us: body(): factor = jnp.linalg.cholesky(gram)]
    another operation x37 -> x0, local copies, waits for them, and re-layouts: 25 us -> none
  transfers between devices with their start and end apart: 6 -> 6, of which waited for: 4 -> 5; matrix products, arithmetic and copies ran while one was open for 45% -> 4% of each run, Pallas kernels for 0% -> 8%
where the time goes in v1:
time: 492 us
  waiting for transfers between devices  380 us (77%)
  Pallas kernels  41.5 us (8%)
  matrix products  28.2 us (6%)
  between operations  13.9 us (3%)
  local copies, waits for them, and re-layouts  11.4 us (2%)
  other arithmetic  11.1 us (2%)
  starting transfers between devices  5.32 us (1%)
    psum x1, waiting for transfers between devices, together(): total = lax.psum(ravelled, axis)  192 us
    all_to_all x1, waiting for transfers between devices, summed_on_arrival(): lax.all_to_all(blocks, axis, split_axis=0, concat_axis=0, tiled=True)  75.7 us
    all_gather x1, waiting for transfers between devices, body(): both = tdot(stacked, lax.all_gather(panel, 'band', axis=0, tiled=True))  56.3 us
    all_gather x1, waiting for transfers between devices, body(): gram = lax.all_gather(gram_part, 'band', axis=0, tiled=True)  48.1 us
    pallas_call x1, Pallas kernels, inverse_factor(): pl.pallas_call(chol_kernel, out_shape=jax.ShapeDtypeStruct((n, n), F32),...  41.5 us
    dot_general x3, matrix products, ndot(): return jnp.dot(left, right, precision=lax.Precision.HIGH)  19.8 us
  transfers between devices with their start and end apart: 6, of which 5 were waited for; matrix products, arithmetic and copies ran while one was open for 4% of the time, Pallas kernels for 8%

profile of v1, /device:TPU:1, one launch (start us, length us, event | category | flops | bytes accessed | tf_op | source)
XLA Modules:
  0.0 491.8 jit_solution(17045039611634238928)
XLA Ops:
  7.2 0.7 all-gather.4.cloned.1.call-update
  7.9 56.3 %all-gather.4.cloned.1.call-done = f32[1024,1024]{1,0:T(8,128)} async-done(((f32[256,1024]{1,0:T(8,128)}), f32[1024,1024]{1,0:T(8,128)}) %all-gather.4.cloned.1.call-update) | async-done | bytes 4194320 | tf_op jit(solution)/shard_map/all_gather | solution.py:153
  64.2 8.4 %fusion = f32[768,1024]{1,0:T(8,128)S(1)} fusion(f32[1024,1024]{1,0:T(8,128)} %all-gather.4.cloned.1.call-done, f32[256,1024]{1,0:T(8,128)} %param.3, f32[512,1024]{1,0:T(8,128)} %param.2), kind=kOutput, calls=%fused_computation | convolution fusion | flops 4832624640 | bytes 10485760 | tf_op jit(solution)/shard_map/dot_general | solution.py:133
  72.9 0.5 copy.6
  73.6 1.8 pad_maximum_fusion
  75.5 191.9 %all-reduce.2.cloned.1.call-done = f32[786432]{0:T(1024)} async-done(((f32[786432]{0:T(1024)}), f32[786432]{0:T(1024)}) %all-reduce.2.cloned.1.call-update) | async-done | bytes 3145744 | tf_op jit(solution)/shard_map/psum | solution.py:114
  267.3 1.7 slice_multiply_fusion
  269.1 1.5 div.21
  270.6 7.7 %fusion.13 = f32[1024,1024]{1,0:T(8,128)} fusion(f32[512,1024]{1,0:T(8,128)} %div.21, f32[512,1024]{1,0:T(8,128)} %param.2), kind=kOutput, calls=%fused_computation.20 | convolution fusion | flops 3221225472 | bytes 8388608 | tf_op jit(solution)/shard_map/dot_general | solution.py:143
  278.3 1.5 reshape.36
  279.8 3.1 copy.5
  282.9 6.6 %fusion.12 = f32[4,256,1024]{2,1,0:T(8,128)} fusion(f32[4,256,512]{2,1,0:T(8,128)} %bitcast.16, f32[512,1024,1]{1,0,2:T(8,128)S(1)} %copy-done.3), kind=kOutput, calls=%fused_computation.19 | convolution fusion | flops 3221225472 | bytes 8388608 | tf_op jit(solution)/shard_map/dot_general | solution.py:143
  289.5 4.9 %all-to-all-start = ((f32[4,256,1024]{2,1,0:T(8,128)}), f32[4,256,1024]{2,1,0:T(8,128)}, u32[]{:S(2)}, u32[]{:S(2)}) async-start(f32[4,256,1024]{2,1,0:T(8,128)} %fusion.12), calls=%async_computation | async-start | bytes 8388608 | tf_op jit(solution)/shard_map/all_to_all | solution.py:128
  294.4 1.3 slice_multiply_fusion.1
  295.9 75.7 %all-to-all-done = f32[4,256,1024]{2,1,0:T(8,128)} async-done(((f32[4,256,1024]{2,1,0:T(8,128)}), f32[4,256,1024]{2,1,0:T(8,128)}, u32[]{:S(2)}, u32[]{:S(2)}) %all-to-all-start) | async-done | bytes 4194336 | tf_op jit(solution)/shard_map/all_to_all | solution.py:128
  371.6 2.7 reduce_sum.9
  374.3 1.2 sub.6
  375.9 2.3 sub.7
  378.3 48.1 %all-gather.6.cloned.1.call-done.g_ref = f32[1024,1024]{1,0:T(8,128)} async-done(((f32[256,1024]{1,0:T(8,128)}), f32[1024,1024]{1,0:T(8,128)}) %all-gather.6.cloned.1.call-update) | async-done | bytes 4194320 | tf_op jit(solution)/shard_map/all_gather | solution.py:160
  426.4 2.2 copy-done.1
  428.6 41.5 %shard_map.41 = f32[1024,1024]{1,0:T(8,128)S(1)} custom-call(f32[1024,1024]{1,0:T(8,128)S(1)} %copy-done.1), custom_call_target="tpu_custom_call" | custom-call | tf_op jit(solution)/shard_map/pallas_call | solution.py:102
  470.0 2.0 copy-done
  472.0 7.8 %all-gather.8.cloned.1.call-done = f32[1024,1024]{1,0:T(8,128)} async-done(((f32[256,1024]{1,0:T(8,128)}), f32[1024,1024]{1,0:T(8,128)}) %all-gather.8.cloned.1.call-update) | async-done | bytes 4194320 | tf_op jit(solution)/shard_map/all_gather | solution.py:166
  479.8 5.5 %fusion.4 = f32[256,1024]{1,0:T(8,128)} fusion(f32[1024,1024]{1,0:T(8,128)} %all-gather.8.cloned.1.call-done, f32[1024,1024]{1,0:T(8,128)} %copy-done, s32[]{:T(128)S(6)} %select_n.7, s32[256]{0:T(256)S(1)} %iota_add_fusion), kind=kOutput, calls=%fused_computation.9 | convolution fusion | flops 1611137024 | bytes 6292484 | tf_op jit(solution)/shard_map/dot_general | solution.py:143
  (21 shorter events, 1.2 us)
Async XLA Ops:
  7.2 57.1 %all-gather.4.cloned.1.call-start = ((), (), s32[]{:S(2)}) async-start(), calls=%async_computation.2 | async-start | bytes 5242880 | tf_op jit(solution)/shard_map/all_gather | solution.py:153
  7.9 259.4 %all-reduce.2.cloned.1.call-start = ((), (), s32[]{:S(2)}) async-start(), calls=%async_computation.3 | async-start | bytes 6291456 | tf_op jit(solution)/shard_map/psum | solution.py:114
  75.4 300.4 %reduce-scatter.2.cloned.1.call-start = ((), (), s32[]{:S(2)}) async-start(), calls=%async_computation.5 | async-start | bytes 5242880 | tf_op jit(solution)/shard_map/reduce_scatter | solution.py:156
  279.8 3.1 copy-start.3
  289.5 82.2 %all-to-all-start = ((f32[4,256,1024]{2,1,0:T(8,128)}), f32[4,256,1024]{2,1,0:T(8,128)}, u32[]{:S(2)}, u32[]{:S(2)}) async-start(f32[4,256,1024]{2,1,0:T(8,128)} %fusion.12), calls=%async_computation | async-start | bytes 8388608 | tf_op jit(solution)/shard_map/all_to_all | solution.py:128
  294.4 132.0 %all-gather.6.cloned.1.call-start = ((), (), s32[]{:S(2)}) async-start(), calls=%async_computation.4 | async-start | bytes 5242880 | tf_op jit(solution)/shard_map/all_gather | solution.py:160
  374.3 1.6 copy-start.2
  375.6 104.2 %all-gather.8.cloned.1.call-start = ((), (), s32[]{:S(2)}) async-start(), calls=%async_computation.6 | async-start | bytes 5242880 | tf_op jit(solution)/shard_map/all_gather | solution.py:166
  426.4 2.2 copy-start.1
  470.0 2.0 copy-start
Sparse Core Ops, SparseCore 0:
  9.8 54.3 all-gather.3
  75.5 191.7 all-reduce.1
  278.4 76.8 reduce-scatter.1
  375.7 50.6 all-gather.5
  428.6 51.1 all-gather.7

commit v2 on v1

--- a/solution.py
+++ b/solution.py
@@ -72,10 +72,17 @@
 
 B = 128
 
+
 def chol_kernel(g_ref, m_ref, th, tl):
-    n = g_ref.shape[0]
+    n = m_ref.shape[0]
     nb = n // B
-    m_ref[...] = g_ref[...]
+    hb = g_ref.shape[0] // 2
+    for t in range(nb // 2):
+        for c in range(2):
+            src = pl.ds(c * hb + t * 64, 64)
+            m_ref[pl.ds(t * B + c * 64, 64), pl.ds(t * B, n - t * B)] = g_ref[src, pl.ds(0, n - t * B)]
+            u = nb - 1 - t
+            m_ref[pl.ds(u * B + c * 64, 64), pl.ds(u * B, n - u * B)] = g_ref[src, pl.ds(n - t * B, n - u * B)]
 
     def step(k, _):
         r = pl.multiple_of(k * B, B)
@@ -96,11 +103,14 @@
         lax.fori_loop(k + 1, nb, rest, 0)
         return 0
     lax.fori_loop(0, nb, step, 0)
-
-def inverse_factor(g):
-    n = g.shape[0]
+    for t in range(nb - 1):
+        m_ref[pl.ds(t * B, B), pl.ds(t * B + B, n - t * B - B)] = jnp.zeros((B, n - t * B - B), F32)
+
+
+def inverse_factor(g, n):
     return pl.pallas_call(
         chol_kernel,
+        name="inverse_factor",
         out_shape=jax.ShapeDtypeStruct((n, n), F32),
         in_specs=[pl.BlockSpec(memory_space=pltpu.VMEM)],
         out_specs=pl.BlockSpec(memory_space=pltpu.VMEM),
@@ -109,34 +119,331 @@
     )(g)
 
 
-def together(arrays, axis):
-    ravelled, at, finished = (jnp.concatenate([a.reshape(-1) for a in arrays]), 0, [])
-    total = lax.psum(ravelled, axis)
-    for a in arrays:
-        finished.append(total[at : at + a.size].reshape(a.shape))
-        at += a.size
-    return tuple(finished)
-
-
-def cut_along(array, dim, count):
-    before, after = (array.shape[:dim], array.shape[dim + 1 :])
-    return jnp.moveaxis(array.reshape(*before, count, -1, *after), dim, 0)
-
-
-def summed_on_arrival(array, axis, dim):
-    blocks = cut_along(array, dim, lax.axis_size(axis))
-    arrived = lax.all_to_all(blocks, axis, split_axis=0, concat_axis=0, tiled=True)
-    return arrived.sum(axis=0)
+MESH = pl.DeviceIdType.MESH
+NX, NZ, NY = 4, 8, 4
+
+
+def place():
+    g = lax.axis_index("grid")
+    return lax.rem(g, 2), lax.rem(lax.div(g, 2), NX), lax.div(g, 2 * NX), lax.axis_index("band")
+
+
+def grid_id(z, x, c):
+    return {"grid": (z * NX + x) * 2 + c}
+
+
+def sender(send, recv):
+    made = []
+
+    def copy(src, dst, device):
+        at = len(made)
+        made.append(
+            pltpu.make_async_remote_copy(
+                src_ref=src, dst_ref=dst, send_sem=send.at[at], recv_sem=recv.at[at],
+                device_id=device, device_id_type=MESH,
+            )
+        )
+        made[-1].start()
+        return made[-1]
+
+    return copy, made
+
+
+def greet(devices):
+    barrier = pltpu.get_barrier_semaphore()
+    for device in devices:
+        pl.semaphore_signal(barrier, inc=1, device_id=device, device_id_type=MESH)
+    pl.semaphore_wait(barrier, len(devices))
+
+
+def rows_of(start, count):
+    return pl.ds(pl.multiple_of(start, 8), count)
+
+
+def lanes_of(start, count):
+    return pl.ds(pl.multiple_of(start, 128), count)
+
+
+def communicate(kernel, name, out_shape, operands, scratch, copies, cid):
+    space = pl.BlockSpec(memory_space=pltpu.VMEM)
+    return pl.pallas_call(
+        kernel,
+        name=name,
+        out_shape=jax.ShapeDtypeStruct(out_shape, F32),
+        in_specs=[space] * len(operands),
+        out_specs=space,
+        scratch_shapes=[pltpu.VMEM(s, F32) for s in scratch]
+        + [pltpu.SemaphoreType.DMA((copies,)), pltpu.SemaphoreType.DMA((copies,))],
+        compiler_params=pltpu.CompilerParams(
+            collective_id=cid, has_side_effects=True, vmem_limit_bytes=48 * 2**20
+        ),
+    )(*operands)
+
+
+def ring_gather(copy, out, base, count, mine, right, left, wrap, size):
+    half = count // 2
+    first = lambda q: out.at[rows_of(base + q * count, half)]
+    second = lambda q: out.at[rows_of(base + q * count + half, half)]
+    a = copy(first(mine), first(mine), right)
+    b = copy(second(mine), second(mine), left)
+    c = copy(second(mine), second(mine), right)
+    d = copy(first(mine), first(mine), left)
+    before, after, far = wrap(mine + size - 1), wrap(mine + 1), wrap(mine + 2)
+    a.wait_recv()
+    e = copy(first(before), first(before), right)
+    b.wait_recv()
+    f = copy(second(after), second(after), left)
+    c.wait_recv()
+    yield before
+    d.wait_recv()
+    yield after
+    e.wait_recv()
+    f.wait_recv()
+    yield far
+
+
+def gather_kernel(p_ref, out, send, recv):
+    _, _, _, y = place()
+    n = p_ref.shape[0]
+    half = n // 2
+    wrap = lambda q: lax.rem(q, NY)
+    right, left = {"band": wrap(y + 1)}, {"band": wrap(y + NY - 1)}
+    greet([right, left])
+    copy, made = sender(send, recv)
+    first = lambda q: out.at[rows_of(q * n, half)]
+    second = lambda q: out.at[rows_of(q * n + half, half)]
+    p1, p2 = p_ref.at[pl.ds(0, half)], p_ref.at[pl.ds(half, half)]
+    a = copy(p1, first(y), right)
+    b = copy(p2, second(y), left)
+    c = copy(p2, second(y), right)
+    d = copy(p1, first(y), left)
+    out[rows_of(y * n, n)] = p_ref[...]
+    a.wait_recv()
+    e = copy(first(wrap(y + NY - 1)), first(wrap(y + NY - 1)), right)
+    b.wait_recv()
+    f = copy(second(wrap(y + 1)), second(wrap(y + 1)), left)
+    for m in (c, d, e, f):
+        m.wait_recv()
+    for m in made:
+        m.wait_send()
+
+
+def gather_band(p):
+    n, w = p.shape
+    return communicate(gather_kernel, "gather_band", (n * NY, w), [p], [], 6, 1)
+
+
+def scatter_kernel(z_ref, base, out, mid, send, recv):
+    _, _, _, y = place()
+    n = base.shape[0]
+    half = n // 2
+    wrap = lambda q: lax.rem(q, NY)
+    right, left = {"band": wrap(y + 1)}, {"band": wrap(y + NY - 1)}
+    before, after, far = wrap(y + NY - 1), wrap(y + 1), wrap(y + 2)
+    greet([right, left])
+    copy, made = sender(send, recv)
+    first = lambda q: rows_of(q * n, half)
+    second = lambda q: rows_of(q * n + half, half)
+    a = copy(z_ref.at[first(far)], mid.at[0], right)
+    b = copy(z_ref.at[second(far)], mid.at[1], left)
+    c = copy(z_ref.at[second(after)], mid.at[2], right)
+    d = copy(z_ref.at[first(before)], mid.at[3], left)
+    a.wait_recv()
+    mid[6] = mid[0] + z_ref[first(after)]
+    e = copy(mid.at[6], mid.at[4], right)
+    b.wait_recv()
+    mid[7] = mid[1] + z_ref[second(before)]
+    f = copy(mid.at[7], mid.at[5], left)
+    c.wait_recv()
+    d.wait_recv()
+    e.wait_recv()
+    out[pl.ds(0, half)] = base[pl.ds(0, half)] - (z_ref[first(y)] + (mid[3] + mid[4]))
+    f.wait_recv()
+    out[pl.ds(half, half)] = base[pl.ds(half, half)] - (z_ref[second(y)] + (mid[2] + mid[5]))
+    for m in made:
+        m.wait_send()
+
+
+def subtract_scattered(z, base):
+    n, w = base.shape
+    return communicate(scatter_kernel, "scatter_band", (n, w), [z, base], [(8, n // 2, w)], 6, 2)
+
+
+def total_kernel(v, out, pair, acc, ring, bz, bx, bfin, bcol, az, afin, send, recv):
+    c, x, z, _ = place()
+    half = v.shape[0] // 2
+    nb = bcol.shape[0]
+    na = half - nb
+    pa, pb = na // NX, nb // NX
+    h = pa // 2
+    wx, wz = (lambda q: lax.rem(q, NX)), (lambda q: lax.rem(q, NZ))
+    other = grid_id(z, x, 1 - c)
+    right, left = grid_id(z, wx(x + 1), c), grid_id(z, wx(x + NX - 1), c)
+    xs = [grid_id(z, wx(x + d), c) for d in range(1, NX)]
+    zs = [grid_id(wz(z + d), x, c) for d in range(1, NZ)]
+    greet([other] + xs + zs)
+    copy, made = sender(send, recv)
+    mine, theirs = c * half, (1 - c) * half
+    B = pl.ds(na, nb)
+    A = pl.ds(0, na)
+    sb = copy(v.at[rows_of(theirs + na, nb)], pair.at[B], other)
+    sa = copy(v.at[rows_of(theirs, na)], pair.at[A], other)
+    sb.wait_recv()
+    acc[B] = v[rows_of(mine + na, nb)] + pair[B]
+    b1 = [copy(acc.at[B, lanes_of(wz(z + d) * 128, 128)], bz.at[d - 1], zs[d - 1]) for d in range(1, NZ)]
+    sa.wait_recv()
+    acc[A] = v[rows_of(mine, na)] + pair[A]
+    up = lambda q: rows_of(q * pa, h)
+    down = lambda q: rows_of(q * pa + h, h)
+    before, after, far = wx(x + NX - 1), wx(x + 1), wx(x + 2)
+    m0 = copy(acc.at[up(far)], ring.at[0], right)
+    m1 = copy(acc.at[down(far)], ring.at[1], left)
+    m2 = copy(acc.at[down(after)], ring.at[2], right)
+    m3 = copy(acc.at[up(before)], ring.at[3], left)
+    m0.wait_recv()
+    ring[6] = acc[up(after)] + ring[0]
+    m4 = copy(ring.at[6], ring.at[4], right)
+    m1.wait_recv()
+    ring[7] = acc[down(before)] + ring[1]
+    m5 = copy(ring.at[7], ring.at[5], left)
+    for m in b1:
+        m.wait_recv()
+    t = acc[B, lanes_of(z * 128, 128)]
+    for d in range(NZ - 1):
+        t = t + bz[d]
+    bfin[...] = t
+    b2 = [copy(bfin.at[rows_of(wx(x + d) * pb, pb)], bx.at[d - 1], xs[d - 1]) for d in range(1, NX)]
+    for m in (m2, m3, m4, m5):
+        m.wait_recv()
+    acc[up(x)] = acc[up(x)] + (ring[3] + ring[4])
+    acc[down(x)] = acc[down(x)] + (ring[2] + ring[5])
+    piece = rows_of(x * pa, pa)
+    a1 = [copy(acc.at[piece, lanes_of(wz(z + d) * 128, 128)], az.at[d - 1], zs[d - 1]) for d in range(1, NZ)]
+    for m in b2:
+        m.wait_recv()
+    bq = rows_of(x * pb, pb)
+    s = bfin[bq, :]
+    for d in range(NX - 1):
+        s = s + bx[d]
+    bcol[bq, :] = s
+    b3 = [copy(bcol.at[bq], bcol.at[bq], xs[d - 1]) for d in range(1, NX)]
+    for m in a1:
+        m.wait_recv()
+    t = acc[piece, lanes_of(z * 128, 128)]
+    for d in range(NZ - 1):
+        t = t + az[d]
+    afin[...] = t
+    cols = lanes_of(z * 128, 128)
+    a2 = [copy(afin, out.at[rows_of(mine + x * pa, pa), cols], zs[d - 1]) for d in range(1, NZ)]
+    out[rows_of(mine + x * pa, pa), cols] = t
+    for m in b3:
+        m.wait_recv()
+    ob = rows_of(mine + na, nb)
+    b4 = [copy(bcol, out.at[ob, cols], zs[d - 1]) for d in range(1, NZ)]
+    out[ob, cols] = bcol[...]
+    for m in a2:
+        m.wait_recv()
+    last = []
+    whole = lambda q: out.at[rows_of(mine + q * pa, pa)]
+    parts = ring_gather(copy, out, mine, pa, x, right, left, wx, NX)
+    got = next(parts)
+    last.append(copy(whole(x), whole(x), other))
+    last.append(copy(whole(got), whole(got), other))
+    got = next(parts)
+    last.append(copy(whole(got), whole(got), other))
+    for m in b4:
+        m.wait_recv()
+    last.append(copy(out.at[ob], out.at[ob], other))
+    got = next(parts)
+    last.append(copy(whole(got), whole(got), other))
+    for m in last:
+        m.wait_recv()
+    for m in made:
+        m.wait_send()
+
+
+def total_grid(v):
+    n, w = v.shape
+    half = n // 2
+    nb = 64
+    pa = (half - nb) // NX
+    scratch = [
+        (half, w), (half, w), (8, pa // 2, w), (NZ - 1, nb, 128), (NX - 1, nb // NX, 128),
+        (nb, 128), (nb, 128), (NZ - 1, pa, 128), (pa, 128),
+    ]
+    return communicate(total_kernel, "total_grid", (n, w), [v], scratch, 2 + 7 + 6 + 3 + 7 + 3 + 7 + 7 + 6 + 5, 3)
+
+
+def gram_kernel(part, out, yb, fin, send, recv):
+    c, x, z, y = place()
+    n = part.shape[0]
+    q = n // NY
+    wx, wy = (lambda q: lax.rem(q, NX)), (lambda q: lax.rem(q, NY))
+    other = grid_id(z, x, 1 - c)
+    xs = [grid_id(z, wx(x + d), c) for d in range(1, NX)]
+    ys = [{"band": wy(y + d)} for d in range(1, NY)]
+    greet([other, xs[0], xs[2]] + ys)
+    copy, made = sender(send, recv)
+    r1 = [copy(part.at[rows_of(wy(y + d) * q, q)], yb.at[d - 1], ys[d - 1]) for d in range(1, NY)]
+    for m in r1:
+        m.wait_recv()
+    t = part[rows_of(y * q, q)]
+    for d in range(NY - 1):
+        t = t + yb[d]
+    fin[...] = t
+    base = c * (n * NX)
+    at = rows_of(base + x * n + y * q, q)
+    r2 = [copy(fin, out.at[at], ys[d - 1]) for d in range(1, NY)]
+    out[at] = t
+    for m in r2:
+        m.wait_recv()
+    whole = lambda b: out.at[rows_of(base + b * n, n)]
+    last = []
+    parts = ring_gather(copy, out, base, n, x, xs[0], xs[2], wx, NX)
+    got = next(parts)
+    last.append(copy(whole(x), whole(x), other))
+    last.append(copy(whole(got), whole(got), other))
+    for got in parts:
+        last.append(copy(whole(got), whole(got), other))
+    for m in last:
+        m.wait_recv()
+    for m in made:
+        m.wait_send()
+
+
+def total_gram(part):
+    n, w = part.shape
+    return communicate(gram_kernel, "total_gram", (2 * NX * n, w), [part], [(NY - 1, n // NY, w), (n // NY, w)], 3 + 3 + 6 + 4, 4)
+
+
+def part_kernel(cf, pp, out, ch, cl, tmp):
+    c, x, _, y = place()
+    ch[...], cl[...] = halves(cf[...])
+    for s in range(9):
+        upper = s < 8 - x
+        rb = jnp.where(upper, x, 7 - x)
+        cb = jnp.where(upper, x + s, s - 1)
+        r, q = lanes_of(rb * 128, 128), lanes_of(cb * 128, 128)
+        prod = dot3((ch[:, r], cl[:, r]), (ch[:, q], cl[:, q]), TN)
+        own = (lax.div(rb, 2) == y).astype(F32)
+        tmp[...] = own * pp[rows_of(lax.rem(rb, 2) * 128, 128), q] - prod
+        out[:, pl.ds(s * 128, 128)] = tmp[rows_of(c * 64, 64), :]
+
+
+def gram_part(cf, pp):
+    space = pl.BlockSpec(memory_space=pltpu.VMEM)
+    return pl.pallas_call(
+        part_kernel,
+        name="gram_part",
+        out_shape=jax.ShapeDtypeStruct((64, 9 * 128), F32),
+        in_specs=[space] * 2,
+        out_specs=space,
+        scratch_shapes=[pltpu.VMEM(cf.shape, BF16), pltpu.VMEM(cf.shape, BF16), pltpu.VMEM((128, 128), F32)],
+    )(cf, pp)
 
 
 def tdot(left, right):
-    return lax.dot_general(
-        left,
-        right,
-        (((1,), (1,)), ((), ())),
-        precision=lax.Precision.HIGH,
-        preferred_element_type=jnp.float32,
-    )
+    return lax.dot_general(left, right, (NT, ((), ())), precision=lax.Precision.HIGH, preferred_element_type=F32)
 
 
 def ndot(left, right):
@@ -145,34 +452,21 @@
 
 def body(basis, panel):
     n_grid = panel.shape[1] * lax.axis_size("grid")
-    n_band = lax.axis_size("band")
-    rows_q = basis.shape[0]
-    rows_p = panel.shape[0]
-    n_panel = rows_p * n_band
-    stacked = jnp.concatenate([basis, panel], 0)
-    both = tdot(stacked, lax.all_gather(panel, "band", axis=0, tiled=True))
-    coeff_sum, gram_sum = together((both[:rows_q], both[rows_q:]), "grid")
-    coeffs = coeff_sum / n_grid
-    projected = panel - lax.psum_scatter(
-        ndot(coeffs.T, basis), "band", scatter_dimension=0, tiled=True
-    )
-    gram_part = gram_sum / n_grid - summed_on_arrival(ndot(coeffs.T, coeffs), "band", 0)
-    gram = lax.all_gather(gram_part, "band", axis=0, tiled=True)
-    offset = lax.axis_index("band") * rows_p
-    inverse_rows = lax.dynamic_slice_in_dim(inverse_factor(gram), offset, rows_p, 0)
-    row_ids = lax.broadcasted_iota(jnp.int32, (rows_p, n_panel), 0)
-    col_ids = lax.broadcasted_iota(jnp.int32, (rows_p, n_panel), 1)
-    inverse_rows = jnp.where(col_ids <= row_ids + offset, inverse_rows, 0.0)
-    new_panel = ndot(inverse_rows, lax.all_gather(projected, "band", axis=0, tiled=True))
+    rows_q, rows_p = basis.shape[0], panel.shape[0]
+    n_panel = rows_p * lax.axis_size("band")
+    whole = gather_band(panel)
+    both = total_grid(tdot(jnp.concatenate([basis, panel], 0), whole))
+    coeffs = both[:rows_q] / n_grid
+    gram = total_gram(gram_part(coeffs, both[rows_q:] / n_grid))
+    inverse = inverse_factor(gram, n_panel)
+    outer = ndot(tdot(inverse, coeffs), basis)
+    rows = lax.dynamic_slice_in_dim(inverse, lax.axis_index("band") * rows_p, rows_p, 0)
+    new_panel = subtract_scattered(outer, ndot(rows, whole))
     return (new_panel, coeffs)
 
 
 def solution(mesh):
     placed = (P("band", "grid"), P("band", "grid"))
     return jax.shard_map(
-        body,
-        mesh=mesh,
-        in_specs=placed,
-        out_specs=(P("band", "grid"), P("band", None)),
-        check_vma=False,
+        body, mesh=mesh, in_specs=placed, out_specs=(P("band", "grid"), P("band", None)), check_vma=False,
     )

time: 492 us -> 243 us (0.49)
  waiting for transfers between devices: 380 us -> 0 us
  Pallas kernels: 41.5 us -> 212 us
  between operations: 13.9 us -> 0.73 us
  other arithmetic: 11.1 us -> 2.71 us
  matrix products: 28.2 us -> 19.9 us
  starting transfers between devices: 5.32 us -> 0 us
    psum x1 -> x0, waiting for transfers between devices: 192 us -> none  [together(): total = lax.psum(ravelled, axis)]
    pallas_call x1 -> x6, Pallas kernels: 41.5 us -> 212 us  [the longest x4 166 us: communicate(): pl.pallas_call(kernel, name=name, out_shape=jax.ShapeDtypeStruct(out_shap...]
    all_gather x3 -> x0, waiting for transfers between devices: 112 us -> none  [the longest x1 56.3 us: body(): both = tdot(stacked, lax.all_gather(panel, 'band', axis=0, tiled=True))]
    all_to_all x1 -> x0, waiting for transfers between devices: 75.7 us -> none  [summed_on_arrival(): lax.all_to_all(blocks, axis, split_axis=0, concat_axis=0, tiled=True)]
    dot_general x3 -> x2, matrix products: 19.8 us -> 9.65 us  [ndot(): return jnp.dot(left, right, precision=lax.Precision.HIGH)]
    all_to_all x1 -> x0, starting transfers between devices: 4.93 us -> none  [summed_on_arrival(): lax.all_to_all(blocks, axis, split_axis=0, concat_axis=0, tiled=True)]
    dot_general x1 -> x2, matrix products: 8.43 us -> 10.2 us  [tdot(): lax.dot_general(left, right, (NT, ((), ())), precision=lax.Precision.HIGH...]
  transfers between devices with their start and end apart: 6 -> 0, of which waited for: 5 -> 0; matrix products, arithmetic and copies ran while one was open for 4% -> 0% of each run, Pallas kernels for 8% -> 0%
where the time goes in v2:
time: 243 us; the launch traced here: 242 us
  Pallas kernels  212 us (87%)
  matrix products  19.9 us (8%)
  local copies, waits for them, and re-layouts  7.07 us (3%)
  other arithmetic  2.71 us (1%)
    pallas_call x4, Pallas kernels, communicate(): pl.pallas_call(kernel, name=name, out_shape=jax.ShapeDtypeStruct(out_shap...  166 us
    pallas_call x1, Pallas kernels, inverse_factor(): pl.pallas_call(chol_kernel, name='inverse_factor', out_shape=jax.ShapeDty...  41.6 us
    dot_general x2, matrix products, tdot(): lax.dot_general(left, right, (NT, ((), ())), precision=lax.Precision.HIGH...  10.2 us
    dot_general x2, matrix products, ndot(): return jnp.dot(left, right, precision=lax.Precision.HIGH)  9.65 us
    unnamed x15, local copies, waits for them, and re-layouts  7.07 us

profile of v2, /device:TPU:1, one launch (start us, length us, event | category | flops | bytes accessed | tf_op | source)
XLA Modules:
  0.0 242.3 jit_solution(7988047296843906301)
XLA Ops:
  0.6 0.0 copy-start.3
  0.6 1.2 copy-done.3
  1.9 0.0 copy-start.6
  1.9 36.8 %gather_band.1 = f32[1024,1024]{1,0:T(8,128)S(1)} custom-call(f32[256,1024]{1,0:T(8,128)S(1)} %copy-done.3), custom_call_target="tpu_custom_call" | custom-call | tf_op jit(solution)/shard_map/gather_band/pallas_call | solution.py:169
  38.6 0.0 copy-start
  38.6 1.9 copy-done
  40.6 0.0 copy-done.6
  40.6 6.8 %fusion.v = f32[768,1024]{1,0:T(8,128)} fusion(f32[1024,1024]{1,0:T(8,128)S(1)} %gather_band.1, f32[256,1024]{1,0:T(8,128)S(1)} %copy-done.3, f32[512,1024]{1,0:T(8,128)S(1)} %copy-done.6), kind=kOutput, calls=%fused_computation | convolution fusion | flops 4832624640 | bytes 10485760 | tf_op jit(solution)/shard_map/dot_general | solution.py:446
  47.3 61.6 %total_grid.1 = f32[768,1024]{1,0:T(8,128)S(1)} custom-call(f32[768,1024]{1,0:T(8,128)} %fusion.v), custom_call_target="tpu_custom_call" | custom-call | tf_op jit(solution)/shard_map/total_grid/pallas_call | solution.py:169
  108.9 1.6 slice_multiply_fusion.cf
  110.6 1.1 slice_multiply_fusion.1.pp
  111.6 4.7 %gram_part.1.part = f32[64,1152]{1,0:T(8,128)} custom-call(f32[512,1024]{1,0:T(8,128)} %slice_multiply_fusion.cf, f32[256,1024]{1,0:T(8,128)} %slice_multiply_fusion.1.pp), custom_call_target="tpu_custom_call" | custom-call | tf_op jit(solution)/shard_map/gram_part/pallas_call | solution.py:435
  116.3 1.0 copy-done.4
  117.3 27.7 %total_gram.1.g_ref = f32[512,1152]{1,0:T(8,128)S(1)} custom-call(f32[64,1152]{1,0:T(8,128)S(1)} %copy-done.4), custom_call_target="tpu_custom_call" | custom-call | tf_op jit(solution)/shard_map/total_gram/pallas_call | solution.py:169
  145.0 41.6 %inverse_factor.1 = f32[1024,1024]{1,0:T(8,128)S(1)} custom-call(f32[512,1152]{1,0:T(8,128)S(1)} %total_gram.1.g_ref), custom_call_target="tpu_custom_call" | custom-call | tf_op jit(solution)/shard_map/inverse_factor/pallas_call | solution.py:111
  186.7 0.0 copy-start.1
  186.7 2.0 copy-done.1
  188.6 4.7 %fusion.4.base = f32[256,1024]{1,0:T(8,128)S(1)} fusion(f32[1024,1024]{1,0:T(8,128)} %copy-done, f32[1024,1024]{1,0:T(8,128)} %copy-done.1, s32[]{:T(128)S(6)} %select_n.3), kind=kOutput, calls=%fused_computation.5 | convolution fusion | flops 1610612736 | bytes 6291460 | tf_op jit(solution)/shard_map/dot_general | solution.py:450
  193.3 0.0 copy-done.2
  193.3 0.0 copy-done.5
  193.3 3.5 %fusion.8 = f32[1024,512]{1,0:T(8,128)S(1)} fusion(f32[1024,1024]{1,0:T(8,128)S(1)} %copy-done.2, f32[512,1024]{1,0:T(8,128)S(1)} %copy-done.5), kind=kOutput, calls=%fused_computation.10 | convolution fusion | flops 3221225472 | bytes 8388608 | tf_op jit(solution)/shard_map/dot_general | solution.py:446
  196.8 5.0 %fusion.9.z_ref = f32[1024,1024]{1,0:T(8,128)} fusion(f32[1024,512]{1,0:T(8,128)S(1)} %fusion.8, f32[512,1024]{1,0:T(8,128)S(1)} %copy-done.6), kind=kOutput, calls=%fused_computation.11 | convolution fusion | flops 3221225472 | bytes 8388608 | tf_op jit(solution)/shard_map/dot_general | solution.py:450
  201.8 39.5 %scatter_band.1 = f32[256,1024]{1,0:T(8,128)S(1)} custom-call(f32[1024,1024]{1,0:T(8,128)} %fusion.9.z_ref, f32[256,1024]{1,0:T(8,128)S(1)} %fusion.4.base), custom_call_target="tpu_custom_call" | custom-call | tf_op jit(solution)/shard_map/scatter_band/pallas_call | solution.py:169
  241.3 1.0 copy.5
  (3 shorter events, 0.0 us)
Async XLA Ops:
  0.6 1.2 copy-start.3
  1.9 38.7 %copy-start.6 = (f32[512,1024]{1,0:T(8,128)S(1)}, f32[512,1024]{1,0:T(8,128)}, u32[]{:S(2)}) copy-start(f32[512,1024]{1,0:T(8,128)} %param.2) | copy-start | bytes 6291460
  38.6 1.9 copy-start
  116.3 1.0 copy-start.4
  186.7 2.0 copy-start.1
  188.6 4.7 %copy-start.2 = (f32[1024,1024]{1,0:T(8,128)S(1)}, f32[1024,1024]{1,0:T(8,128)}, u32[]{:S(2)}) copy-start(f32[1024,1024]{1,0:T(8,128)} %copy-done.1) | copy-start | bytes 12582916
  188.6 4.7 %copy-start.5 = (f32[512,1024]{1,0:T(8,128)S(1)}, f32[512,1024]{1,0:T(8,128)}, u32[]{:S(2)}) copy-start(f32[512,1024]{1,0:T(8,128)} %slice_multiply_fusion.cf) | copy-start | bytes 6291460

commit v3 on v2

--- a/solution.py
+++ b/solution.py
@@ -1,3 +1,5 @@
+import functools
+
 import jax
 import jax.numpy as jnp
 from jax import lax
@@ -73,7 +75,10 @@
 B = 128
 
 
-def chol_kernel(g_ref, m_ref, th, tl):
+SCATTERED_AT, PASSED_AT = 3, 6
+
+
+def factorize(g_ref, m_ref, th, tl, between):
     n = m_ref.shape[0]
     nb = n // B
     hb = g_ref.shape[0] // 2
@@ -101,22 +106,12 @@
             m_ref[pl.ds(q, B), :] = m_ref[pl.ds(q, B), :] - dot3(f, (th[...], tl[...]), TN)
             return 0
         lax.fori_loop(k + 1, nb, rest, 0)
+        for when, act in between.items():
+            pl.when(k == when)(act)
         return 0
     lax.fori_loop(0, nb, step, 0)
     for t in range(nb - 1):
         m_ref[pl.ds(t * B, B), pl.ds(t * B + B, n - t * B - B)] = jnp.zeros((B, n - t * B - B), F32)
-
-
-def inverse_factor(g, n):
-    return pl.pallas_call(
-        chol_kernel,
-        name="inverse_factor",
-        out_shape=jax.ShapeDtypeStruct((n, n), F32),
-        in_specs=[pl.BlockSpec(memory_space=pltpu.VMEM)],
-        out_specs=pl.BlockSpec(memory_space=pltpu.VMEM),
-        scratch_shapes=[pltpu.VMEM((B, n), BF16), pltpu.VMEM((B, n), BF16)],
-        compiler_params=pltpu.CompilerParams(vmem_limit_bytes=40 * 2**20),
-    )(g)
 
 
 MESH = pl.DeviceIdType.MESH
@@ -233,43 +228,7 @@
     return communicate(gather_kernel, "gather_band", (n * NY, w), [p], [], 6, 1)
 
 
-def scatter_kernel(z_ref, base, out, mid, send, recv):
-    _, _, _, y = place()
-    n = base.shape[0]
-    half = n // 2
-    wrap = lambda q: lax.rem(q, NY)
-    right, left = {"band": wrap(y + 1)}, {"band": wrap(y + NY - 1)}
-    before, after, far = wrap(y + NY - 1), wrap(y + 1), wrap(y + 2)
-    greet([right, left])
-    copy, made = sender(send, recv)
-    first = lambda q: rows_of(q * n, half)
-    second = lambda q: rows_of(q * n + half, half)
-    a = copy(z_ref.at[first(far)], mid.at[0], right)
-    b = copy(z_ref.at[second(far)], mid.at[1], left)
-    c = copy(z_ref.at[second(after)], mid.at[2], right)
-    d = copy(z_ref.at[first(before)], mid.at[3], left)
-    a.wait_recv()
-    mid[6] = mid[0] + z_ref[first(after)]
-    e = copy(mid.at[6], mid.at[4], right)
-    b.wait_recv()
-    mid[7] = mid[1] + z_ref[second(before)]
-    f = copy(mid.at[7], mid.at[5], left)
-    c.wait_recv()
-    d.wait_recv()
-    e.wait_recv()
-    out[pl.ds(0, half)] = base[pl.ds(0, half)] - (z_ref[first(y)] + (mid[3] + mid[4]))
-    f.wait_recv()
-    out[pl.ds(half, half)] = base[pl.ds(half, half)] - (z_ref[second(y)] + (mid[2] + mid[5]))
-    for m in made:
-        m.wait_send()
-
-
-def subtract_scattered(z, base):
-    n, w = base.shape
-    return communicate(scatter_kernel, "scatter_band", (n, w), [z, base], [(8, n // 2, w)], 6, 2)
-
-
-def total_kernel(v, out, pair, acc, ring, bz, bx, bfin, bcol, az, afin, send, recv):
+def total_kernel(scale, v, out, pair, acc, ring, bz, bx, bfin, bcol, az, afin, send, recv):
     c, x, z, _ = place()
     half = v.shape[0] // 2
     nb = bcol.shape[0]
@@ -325,13 +284,14 @@
     s = bfin[bq, :]
     for d in range(NX - 1):
         s = s + bx[d]
-    bcol[bq, :] = s
+    bcol[bq, :] = s * scale
     b3 = [copy(bcol.at[bq], bcol.at[bq], xs[d - 1]) for d in range(1, NX)]
     for m in a1:
         m.wait_recv()
     t = acc[piece, lanes_of(z * 128, 128)]
     for d in range(NZ - 1):
         t = t + az[d]
+    t = t * scale
     afin[...] = t
     cols = lanes_of(z * 128, 128)
     a2 = [copy(afin, out.at[rows_of(mine + x * pa, pa), cols], zs[d - 1]) for d in range(1, NZ)]
@@ -362,7 +322,7 @@
         m.wait_send()
 
 
-def total_grid(v):
+def total_grid(v, scale):
     n, w = v.shape
     half = n // 2
     nb = 64
@@ -371,54 +331,13 @@
         (half, w), (half, w), (8, pa // 2, w), (NZ - 1, nb, 128), (NX - 1, nb // NX, 128),
         (nb, 128), (nb, 128), (NZ - 1, pa, 128), (pa, 128),
     ]
-    return communicate(total_kernel, "total_grid", (n, w), [v], scratch, 2 + 7 + 6 + 3 + 7 + 3 + 7 + 7 + 6 + 5, 3)
-
-
-def gram_kernel(part, out, yb, fin, send, recv):
-    c, x, z, y = place()
-    n = part.shape[0]
-    q = n // NY
-    wx, wy = (lambda q: lax.rem(q, NX)), (lambda q: lax.rem(q, NY))
-    other = grid_id(z, x, 1 - c)
-    xs = [grid_id(z, wx(x + d), c) for d in range(1, NX)]
-    ys = [{"band": wy(y + d)} for d in range(1, NY)]
-    greet([other, xs[0], xs[2]] + ys)
-    copy, made = sender(send, recv)
-    r1 = [copy(part.at[rows_of(wy(y + d) * q, q)], yb.at[d - 1], ys[d - 1]) for d in range(1, NY)]
-    for m in r1:
-        m.wait_recv()
-    t = part[rows_of(y * q, q)]
-    for d in range(NY - 1):
-        t = t + yb[d]
-    fin[...] = t
-    base = c * (n * NX)
-    at = rows_of(base + x * n + y * q, q)
-    r2 = [copy(fin, out.at[at], ys[d - 1]) for d in range(1, NY)]
-    out[at] = t
-    for m in r2:
-        m.wait_recv()
-    whole = lambda b: out.at[rows_of(base + b * n, n)]
-    last = []
-    parts = ring_gather(copy, out, base, n, x, xs[0], xs[2], wx, NX)
-    got = next(parts)
-    last.append(copy(whole(x), whole(x), other))
-    last.append(copy(whole(got), whole(got), other))
-    for got in parts:
-        last.append(copy(whole(got), whole(got), other))
-    for m in last:
-        m.wait_recv()
-    for m in made:
-        m.wait_send()
-
-
-def total_gram(part):
-    n, w = part.shape
-    return communicate(gram_kernel, "total_gram", (2 * NX * n, w), [part], [(NY - 1, n // NY, w), (n // NY, w)], 3 + 3 + 6 + 4, 4)
-
-
-def part_kernel(cf, pp, out, ch, cl, tmp):
+    return communicate(functools.partial(total_kernel, scale), "total_grid", (n, w), [v], scratch, 2 + 7 + 6 + 3 + 7 + 3 + 7 + 7 + 6 + 5, 3)
+
+
+def part_kernel(both, out, ch, cl, tmp):
     c, x, _, y = place()
-    ch[...], cl[...] = halves(cf[...])
+    nq = ch.shape[0]
+    ch[...], cl[...] = halves(both[pl.ds(0, nq)])
     for s in range(9):
         upper = s < 8 - x
         rb = jnp.where(upper, x, 7 - x)
@@ -426,20 +345,149 @@
         r, q = lanes_of(rb * 128, 128), lanes_of(cb * 128, 128)
         prod = dot3((ch[:, r], cl[:, r]), (ch[:, q], cl[:, q]), TN)
         own = (lax.div(rb, 2) == y).astype(F32)
-        tmp[...] = own * pp[rows_of(lax.rem(rb, 2) * 128, 128), q] - prod
+        tmp[...] = own * both[rows_of(nq + lax.rem(rb, 2) * 128, 128), q] - prod
         out[:, pl.ds(s * 128, 128)] = tmp[rows_of(c * 64, 64), :]
 
 
-def gram_part(cf, pp):
+def gram_part(both, nq):
     space = pl.BlockSpec(memory_space=pltpu.VMEM)
+    w = both.shape[1]
     return pl.pallas_call(
         part_kernel,
         name="gram_part",
         out_shape=jax.ShapeDtypeStruct((64, 9 * 128), F32),
-        in_specs=[space] * 2,
+        in_specs=[space],
         out_specs=space,
-        scratch_shapes=[pltpu.VMEM(cf.shape, BF16), pltpu.VMEM(cf.shape, BF16), pltpu.VMEM((128, 128), F32)],
-    )(cf, pp)
+        scratch_shapes=[pltpu.VMEM((nq, w), BF16), pltpu.VMEM((nq, w), BF16), pltpu.VMEM((128, 128), F32)],
+    )(both)
+
+
+def finish_kernel(part, s_ref, p_ref, out, g, m_ref, yb, fin, mid, whole, th, tl, send, recv):
+    c, x, z, y = place()
+    wx, wy = (lambda q: lax.rem(q, NX)), (lambda q: lax.rem(q, NY))
+    other = grid_id(z, x, 1 - c)
+    xr, xl = grid_id(z, wx(x + 1), c), grid_id(z, wx(x + NX - 1), c)
+    ys = [{"band": wy(y + d)} for d in range(1, NY)]
+    right, left = ys[0], ys[2]
+    before, after, far = wy(y + NY - 1), wy(y + 1), wy(y + 2)
+    greet([other, xr, xl] + ys)
+    made = []
+
+    def plan(src, dst, device):
+        at = len(made)
+        made.append(
+            pltpu.make_async_remote_copy(
+                src_ref=src, dst_ref=dst, send_sem=send.at[at], recv_sem=recv.at[at],
+                device_id=device, device_id_type=MESH,
+            )
+        )
+        return made[-1]
+
+    def copy(src, dst, device):
+        p = plan(src, dst, device)
+        p.start()
+        return p
+
+    n = p_ref.shape[0]
+    h, w4 = n // 2, n // 4
+    first = lambda q: rows_of(q * n, h)
+    second = lambda q: rows_of(q * n + h, h)
+    ng = part.shape[0]
+    q = ng // NY
+    r1 = [copy(part.at[rows_of(wy(y + d) * q, q)], yb.at[d - 1], ys[d - 1]) for d in (2, 1, 3)]
+    a = [copy(s_ref.at[rows_of(far * n + i * w4, w4)], mid.at[0, pl.ds(i * w4, w4)], right) for i in range(1)]
+    b = [copy(s_ref.at[rows_of(far * n + h + i * w4, w4)], mid.at[1, pl.ds(i * w4, w4)], left) for i in range(1)]
+    for m in r1:
+        m.wait_recv()
+    t = part[rows_of(y * q, q)]
+    for d in range(NY - 1):
+        t = t + yb[d]
+    fin[...] = t
+    base = c * (ng * NX)
+    at = rows_of(base + x * ng + y * q, q)
+    r2 = [copy(fin, g.at[at], ys[d - 1]) for d in (2, 1, 3)]
+    a += [copy(s_ref.at[rows_of(far * n + i * w4, w4)], mid.at[0, pl.ds(i * w4, w4)], right) for i in range(1, 2)]
+    b += [copy(s_ref.at[rows_of(far * n + h + i * w4, w4)], mid.at[1, pl.ds(i * w4, w4)], left) for i in range(1, 2)]
+    cc = copy(s_ref.at[second(after)], mid.at[2], right)
+    dd = copy(s_ref.at[first(before)], mid.at[3], left)
+    g[at] = t
+    for m in r2:
+        m.wait_recv()
+    block = lambda b: g.at[rows_of(base + b * ng, ng)]
+    last = []
+    parts = ring_gather(copy, g, base, ng, x, xr, xl, wx, NX)
+    got = next(parts)
+    last.append(copy(block(x), block(x), other))
+    last.append(copy(block(got), block(got), other))
+    for got in parts:
+        last.append(copy(block(got), block(got), other))
+    for m in a:
+        m.wait_recv()
+    mid[6] = mid[0] + s_ref[first(after)]
+    ee = copy(mid.at[6], mid.at[4], right)
+    for m in b:
+        m.wait_recv()
+    mid[7] = mid[1] + s_ref[second(before)]
+    ff = copy(mid.at[7], mid.at[5], left)
+    for m in last:
+        m.wait_recv()
+    up = lambda b: whole.at[first(b)]
+    down = lambda b: whole.at[second(b)]
+    own = [
+        plan(up(y), up(y), right), plan(down(y), down(y), left),
+        plan(down(y), down(y), right), plan(up(y), up(y), left),
+    ]
+    pass_on = [plan(up(before), up(before), right), plan(down(after), down(after), left)]
+
+    def scattered():
+        for m in (cc, dd, ee):
+            m.wait_recv()
+        whole[first(y)] = p_ref[pl.ds(0, h)] - (s_ref[first(y)] + (mid[3] + mid[4]))
+        own[0].start()
+        ff.wait_recv()
+        whole[second(y)] = p_ref[pl.ds(h, h)] - (s_ref[second(y)] + (mid[2] + mid[5]))
+        for m in own[1:]:
+            m.start()
+
+    def passed():
+        for i in range(2):
+            own[i].wait_recv()
+            pass_on[i].start()
+
+    factorize(g, m_ref, th, tl, {SCATTERED_AT: scattered, PASSED_AT: passed})
+
+    def product(b):
+        return dot3(halves(m_ref[rows_of(y * n, n), lanes_of(b * n, n)]), halves(whole[rows_of(b * n, n), :]), NN)
+
+    out[...] = product(y)
+    own[2].wait_recv()
+    out[...] = out[...] + product(before)
+    own[3].wait_recv()
+    out[...] = out[...] + product(after)
+    for m in pass_on:
+        m.wait_recv()
+    out[...] = out[...] + product(far)
+    for m in made:
+        m.wait_send()
+
+
+def finish(part, s, p):
+    n, w = p.shape
+    ng, wg = part.shape
+    total = n * NY
+    space = pl.BlockSpec(memory_space=pltpu.VMEM)
+    shapes = [(2 * NX * ng, wg), (total, total), (NY - 1, ng // NY, wg), (ng // NY, wg), (8, n // 2, w), (total, w)]
+    return pl.pallas_call(
+        finish_kernel,
+        name="finish",
+        out_shape=jax.ShapeDtypeStruct((n, w), F32),
+        in_specs=[space] * 3,
+        out_specs=space,
+        scratch_shapes=[pltpu.VMEM(s_, F32) for s_ in shapes]
+        + [pltpu.VMEM((B, total), BF16)] * 2
+        + [pltpu.SemaphoreType.DMA((30,)), pltpu.SemaphoreType.DMA((30,))],
+        compiler_params=pltpu.CompilerParams(collective_id=5, has_side_effects=True, vmem_limit_bytes=56 * 2**20),
+    )(part, s, p)
 
 
 def tdot(left, right):
@@ -452,16 +500,12 @@
 
 def body(basis, panel):
     n_grid = panel.shape[1] * lax.axis_size("grid")
-    rows_q, rows_p = basis.shape[0], panel.shape[0]
-    n_panel = rows_p * lax.axis_size("band")
+    rows_q = basis.shape[0]
     whole = gather_band(panel)
-    both = total_grid(tdot(jnp.concatenate([basis, panel], 0), whole))
-    coeffs = both[:rows_q] / n_grid
-    gram = total_gram(gram_part(coeffs, both[rows_q:] / n_grid))
-    inverse = inverse_factor(gram, n_panel)
-    outer = ndot(tdot(inverse, coeffs), basis)
-    rows = lax.dynamic_slice_in_dim(inverse, lax.axis_index("band") * rows_p, rows_p, 0)
-    new_panel = subtract_scattered(outer, ndot(rows, whole))
+    both = total_grid(tdot(jnp.concatenate([basis, panel], 0), whole), 1.0 / n_grid)
+    coeffs = both[:rows_q]
+    outer = ndot(coeffs.T, basis)
+    new_panel = finish(gram_part(both, rows_q), outer, panel)
     return (new_panel, coeffs)
 
 

time: 243 us -> 219 us (0.901)
  Pallas kernels: 212 us -> 199 us
  matrix products: 19.9 us -> 12 us
  other arithmetic: 2.71 us -> 0 us
    pallas_call x4 -> x2, Pallas kernels: 166 us -> 98.5 us  [communicate(): pl.pallas_call(kernel, name=name, out_shape=jax.ShapeDtypeStruct(out_shap...]
    pallas_call x1, Pallas kernels: 41.6 us -> 95.5 us  [finish(): pl.pallas_call(finish_kernel, name='finish', out_shape=jax.ShapeDtypeStru...]
    dot_general x2 -> x1, matrix products: 9.65 us -> 5.23 us  [ndot(): return jnp.dot(left, right, precision=lax.Precision.HIGH)]
    dot_general x2 -> x1, matrix products: 10.2 us -> 6.75 us  [tdot(): lax.dot_general(left, right, (NT, ((), ())), precision=lax.Precision.HIGH...]
    div x2 -> x0, other arithmetic: 2.71 us -> none  [the longest x1 1.62 us: body(): coeffs = both[:rows_q] / n_grid]
    unnamed x15 -> x9, local copies, waits for them, and re-layouts: 7.07 us -> 5.18 us
where the time goes in v3:
time: 219 us; the launch traced here: 218 us
  Pallas kernels  199 us (91%)
  matrix products  12 us (5%)
  local copies, waits for them, and re-layouts  7 us (3%)
    pallas_call x2, Pallas kernels, communicate(): pl.pallas_call(kernel, name=name, out_shape=jax.ShapeDtypeStruct(out_shap...  98.5 us
    pallas_call x1, Pallas kernels, finish(): pl.pallas_call(finish_kernel, name='finish', out_shape=jax.ShapeDtypeStru...  95.5 us
    dot_general x1, matrix products, tdot(): lax.dot_general(left, right, (NT, ((), ())), precision=lax.Precision.HIGH...  6.75 us
    dot_general x1, matrix products, ndot(): return jnp.dot(left, right, precision=lax.Precision.HIGH)  5.23 us
    unnamed x9, local copies, waits for them, and re-layouts  5.18 us
    pallas_call x1, Pallas kernels, gram_part(): pl.pallas_call(part_kernel, name='gram_part', out_shape=jax.ShapeDtypeStr...  4.74 us

profile of v3, /device:TPU:1, one launch (start us, length us, event | category | flops | bytes accessed | tf_op | source)
XLA Modules:
  0.0 218.4 jit_solution(12474623003290442925)
XLA Ops:
  0.6 0.0 copy-start.1
  0.6 1.2 copy-done.1
  1.9 0.0 copy-start.2
  1.9 36.8 %gather_band.1 = f32[1024,1024]{1,0:T(8,128)S(1)} custom-call(f32[256,1024]{1,0:T(8,128)S(1)} %copy-done.1), custom_call_target="tpu_custom_call" | custom-call | tf_op jit(solution)/shard_map/gather_band/pallas_call | solution.py:164
  38.6 0.0 copy-done.2
  38.6 6.7 %fusion.v = f32[768,1024]{1,0:T(8,128)} fusion(f32[1024,1024]{1,0:T(8,128)S(1)} %gather_band.1, f32[256,1024]{1,0:T(8,128)S(1)} %copy-done.1, f32[512,1024]{1,0:T(8,128)S(1)} %copy-done.2), kind=kOutput, calls=%fused_computation | convolution fusion | flops 4832624640 | bytes 10485760 | tf_op jit(solution)/shard_map/dot_general | solution.py:494
  45.4 61.7 %total_grid.1.both = f32[768,1024]{1,0:T(8,128)S(1)} custom-call(f32[768,1024]{1,0:T(8,128)} %fusion.v), custom_call_target="tpu_custom_call" | custom-call | tf_op jit(solution)/shard_map/total_grid/pallas_call | solution.py:164
  107.1 0.0 copy-start
  107.1 1.6 copy-done
  108.8 4.7 %gram_part.1.part = f32[64,1152]{1,0:T(8,128)} custom-call(f32[768,1024]{1,0:T(8,128)} %copy-done), custom_call_target="tpu_custom_call" | custom-call | tf_op jit(solution)/shard_map/gram_part/pallas_call | solution.py:355
  113.5 1.8 slice.3
  115.3 0.0 copy-start.3
  115.3 5.2 %fusion.5.s_ref = f32[1024,1024]{1,0:T(8,128)} fusion(f32[512,1024]{1,0:T(8,128)S(1)} %slice.3, f32[512,1024]{1,0:T(8,128)S(1)} %copy-done.2), kind=kOutput, calls=%fused_computation.5 | convolution fusion | flops 3221225472 | bytes 8388608 | tf_op jit(solution)/shard_map/dot_general | solution.py:498
  120.6 0.0 copy-done.3
  120.6 95.5 %finish.1 = f32[256,1024]{1,0:T(8,128)} custom-call(f32[64,1152]{1,0:T(8,128)} %gram_part.1.part, f32[1024,1024]{1,0:T(8,128)} %fusion.5.s_ref, f32[256,1024]{1,0:T(8,128)} %p_ref.3), custom_call_target="tpu_custom_call" | custom-call | tf_op jit(solution)/shard_map/finish/pallas_call | solution.py:480
  216.1 2.3 %copy.5 = f32[256,1024]{1,0:T(8,128)} copy(f32[256,1024]{1,0:T(8,128)} %finish.1) | data formatting | bytes 2097152
Async XLA Ops:
  0.6 1.2 copy-start.1
  1.9 36.8 %copy-start.2 = (f32[512,1024]{1,0:T(8,128)S(1)}, f32[512,1024]{1,0:T(8,128)}, u32[]{:S(2)}) copy-start(f32[512,1024]{1,0:T(8,128)} %param.2) | copy-start | bytes 6291460
  107.1 1.6 copy-start
  115.3 5.2 %copy-start.3 = (f32[512,1024]{1,0:T(8,128)}, f32[512,1024]{1,0:T(8,128)S(1)}, u32[]{:S(2)}) copy-start(f32[512,1024]{1,0:T(8,128)S(1)} %slice.3) | copy-start | bytes 6291460

commit v4 on v1

v4 whole, which is shorter than its diff:
```python
import functools

import jax
import jax.numpy as jnp
from jax import lax
from jax.experimental import pallas as pl
from jax.experimental.pallas import tpu as pltpu
from jax.sharding import PartitionSpec as P

F32, BF16 = jnp.float32, jnp.bfloat16

def halves(x):
    hi = x.astype(BF16)
    return hi, (x - hi.astype(F32)).astype(BF16)

def dot3(a, b, dims):
    (ah, al), (bh, bl) = a, b
    dg = lambda u, v: lax.dot_general(u, v, (dims, ((), ())), preferred_element_type=F32)
    return dg(ah, bh) + (dg(ah, bl) + dg(al, bh))

NN, TN, NT = ((1,), (0,)), ((0,), (0,)), ((1,), (1,))
BASE = 32

def base_block(w, at):
    n = w.shape[0]
    rows = w[at:at + BASE]
    lane = lax.broadcasted_iota(jnp.int32, (BASE, n), 1)
    sub = lax.broadcasted_iota(jnp.int32, (BASE, n), 0)
    cols = []
    for j in range(BASE):
        lo = j // 8 * 8
        cols.append(jnp.broadcast_to(rows[lo:, at + j:at + j + 1], (BASE - lo, n)))
    inside = (lane >= at) & (lane < at + BASE)
    v = jnp.where(inside, (lane == sub + at).astype(F32), rows)
    v = [v[8 * s:8 * s + 8] for s in range(BASE // 8)]
    cols = [[c[8 * s:8 * s + 8] for s in range(c.shape[0] // 8)] for c in cols]
    nb = BASE // 8
    sub8 = lax.broadcasted_iota(jnp.int32, (8, n), 0)
    bc = lambda x, i: jnp.broadcast_to(x[i:i + 1], (8, n))
    for j in range(BASE):
        s0, r0 = j // 8, j % 8
        c = cols[j]
        inv = lax.rsqrt(bc(c[0], r0))
        l = [x * inv for x in c]
        for jj in range(j + 1, BASE):
            s1, r1 = jj // 8, jj % 8
            f = bc(l[s1 - s0], r1)
            for s in range(s1, nb):
                cols[jj][s - s1] = cols[jj][s - s1] - l[s - s0] * f
        piv = bc(v[s0], r0) * inv
        l0 = jnp.where(sub8 > r0, l[0], 0.0)
        v[s0] = jnp.where(sub8 == r0, piv, v[s0] - l0 * piv)
        for s in range(s0 + 1, nb):
            v[s] = v[s] - l[s - s0] * piv
    return jnp.concatenate(v, 0)

def factor128(w):
    n = w.shape[0]
    lane = lax.broadcasted_iota(jnp.int32, (n, n), 1)
    row = lax.broadcasted_iota(jnp.int32, (n, n), 0)
    for at in range(0, n, BASE):
        v = base_block(w, at)
        end = at + BASE
        if end < n:
            parts = halves(v)
            upd = lax.dot_general(v, v, (TN, ((), ())), precision=lax.Precision.HIGHEST, preferred_element_type=F32)
            below = w[end:]
            l2 = lane[end:]
            below = jnp.where((l2 >= at) & (l2 < end), 0.0, below) - upd[end:]
            w = jnp.concatenate(([w[:at]] if at else []) + [v, below], 0)
        else:
            w = jnp.concatenate([w[:at], v], 0)
    return jnp.where(lane <= row, w, 0.0)

B = 128


SCATTERED_AT, PASSED_AT = 0, 3


def factorize(g_ref, m_ref, th, tl, between):
    n = m_ref.shape[0]
    nb = n // B
    hb = g_ref.shape[0] // 2
    for t in range(nb // 2):
        for c in range(2):
            src = pl.ds(c * hb + t * 64, 64)
            m_ref[pl.ds(t * B + c * 64, 64), pl.ds(t * B, n - t * B)] = g_ref[src, pl.ds(0, n - t * B)]
            u = nb - 1 - t
            m_ref[pl.ds(u * B + c * 64, 64), pl.ds(u * B, n - u * B)] = g_ref[src, pl.ds(n - t * B, n - u * B)]

    def step(k, _):
        r = pl.multiple_of(k * B, B)
        inv = factor128(m_ref[pl.ds(r, B), pl.ds(r, B)])
        t = dot3(halves(inv), halves(m_ref[pl.ds(r, B), :]), NN)
        m_ref[pl.ds(r, B), :] = t
        m_ref[pl.ds(r, B), pl.ds(r, B)] = inv
        hi, lo = halves(m_ref[pl.ds(r, B), :])
        th[...] = hi
        tl[...] = lo

        def rest(i, _):
            q = pl.multiple_of(i * B, B)
            m_ref[pl.ds(q, B), pl.ds(r, B)] = jnp.zeros((B, B), F32)
            f = (th[:, pl.ds(q, B)], tl[:, pl.ds(q, B)])
            m_ref[pl.ds(q, B), :] = m_ref[pl.ds(q, B), :] - dot3(f, (th[...], tl[...]), TN)
            return 0
        lax.fori_loop(k + 1, nb, rest, 0)
        for when, act in between.items():
            pl.when(k == when)(act)
        return 0
    lax.fori_loop(0, nb, step, 0)
    for t in range(nb - 1):
        m_ref[pl.ds(t * B, B), pl.ds(t * B + B, n - t * B - B)] = jnp.zeros((B, n - t * B - B), F32)


MESH = pl.DeviceIdType.MESH
NX, NZ, NY = 4, 8, 4


def place():
    g = lax.axis_index("grid")
    return lax.rem(g, 2), lax.rem(lax.div(g, 2), NX), lax.div(g, 2 * NX), lax.axis_index("band")


def grid_id(z, x, c):
    return {"grid": (z * NX + x) * 2 + c}


def sender(send, recv):
    made = []

    def plan(src, dst, device):
        at = len(made)
        made.append(
            pltpu.make_async_remote_copy(
                src_ref=src, dst_ref=dst, send_sem=send.at[at], recv_sem=recv.at[at],
                device_id=device, device_id_type=MESH,
            )
        )
        return made[-1]

    def copy(src, dst, device):
        started = plan(src, dst, device)
        started.start()
        return started

    return plan, copy, made


def greet(devices):
    barrier = pltpu.get_barrier_semaphore()
    for device in devices:
        pl.semaphore_signal(barrier, inc=1, device_id=device, device_id_type=MESH)
    pl.semaphore_wait(barrier, len(devices))


def rows_of(start, count):
    return pl.ds(pl.multiple_of(start, 8), count)


def lanes_of(start, count):
    return pl.ds(pl.multiple_of(start, 128), count)


def ring_gather(copy, out, base, count, mine, right, left, wrap, size):
    half = count // 2
    first = lambda q: out.at[rows_of(base + q * count, half)]
    second = lambda q: out.at[rows_of(base + q * count + half, half)]
    a = copy(first(mine), first(mine), right)
    b = copy(second(mine), second(mine), left)
    c = copy(second(mine), second(mine), right)
    d = copy(first(mine), first(mine), left)
    before, after, far = wrap(mine + size - 1), wrap(mine + 1), wrap(mine + 2)
    a.wait_recv()
    e = copy(first(before), first(before), right)
    b.wait_recv()
    f = copy(second(after), second(after), left)
    c.wait_recv()
    yield before
    d.wait_recv()
    yield after
    e.wait_recv()
    f.wait_recv()
    yield far


def step_kernel(
    scale, q_ref, p_ref, out, coeffs, wh, wl, ch, cl, th, tl, pg, v, pair, acc, ring, zb, zfin, fin,
    pp, ct, rs, part, s_ref, g, m_ref, yb, gfin, mid, whole, send, recv,
):
    c, x, z, y = place()
    nq, npan = q_ref.shape[0], p_ref.shape[0]
    half = v.shape[1] // 2
    pa = half // NX
    h = pa // 2
    zrow = pa // (NZ // 2)
    wx, wz, wy = (lambda q: lax.rem(q, NX)), (lambda q: lax.rem(q, NZ)), (lambda q: lax.rem(q, NY))
    other = grid_id(z, x, 1 - c)
    right, left = grid_id(z, wx(x + 1), c), grid_id(z, wx(x + NX - 1), c)
    zs = [grid_id(wz(z + d), x, c) for d in range(1, NZ)]
    north, south = {"band": wy(y + 1)}, {"band": wy(y + NY - 1)}
    ys = [{"band": lax.rem(y + d, NY)} for d in range(1, NY)]
    greet([other, right, left] + ys + zs)
    plan, copy, made = sender(send, recv)
    mine, theirs = c * half, (1 - c) * half
    xb, xa, xf = wx(x + NX - 1), wx(x + 1), wx(x + 2)
    yb_, ya, yf = wy(y + NY - 1), wy(y + 1), wy(y + 2)
    hp = npan // 2
    p1, p2 = p_ref.at[pl.ds(0, hp)], p_ref.at[pl.ds(hp, hp)]
    gs = [copy(p1, pg.at[0], north), copy(p2, pg.at[1], south), copy(p2, pg.at[2], north), copy(p1, pg.at[3], south)]
    at = [
        (y * npan, y * npan + hp), (yb_ * npan, ya * npan + hp),
        (yb_ * npan + hp, ya * npan), (yf * npan, yf * npan + hp),
    ]
    wh[pl.ds(0, nq)], wl[pl.ds(0, nq)] = halves(q_ref[...])
    wh[pl.ds(nq, npan)], wl[pl.ds(nq, npan)] = halves(p_ref[...])
    n = wh.shape[0]
    tile = 256

    def product(s, rows):
        ph, plo = halves(rows)

        def some(i, _):
            r = rows_of(i * tile, tile)
            v[s, r, :] = dot3((wh[r, :], wl[r, :]), (ph, plo), NT)
            return 0

        lax.fori_loop(0, n // tile, some, 0)

    st = [dict() for _ in range(4)]
    piece = lambda q: rows_of(q * pa, pa)
    up = lambda q: rows_of(q * pa, h)
    down = lambda q: rows_of(q * pa + h, h)
    zpart = lambda q: (rows_of(x * pa + lax.div(q, 2) * zrow, zrow), lanes_of(lax.rem(q, 2) * 128, 128))

    def s0(s):
        if s == 0:
            product(0, p_ref[...])
        else:
            if s == 1:
                gs[0].wait_recv()
                gs.append(copy(pg.at[0], pg.at[4], north))
                gs[1].wait_recv()
                gs.append(copy(pg.at[1], pg.at[5], south))
            else:
                gs[2 * s - 2].wait_recv()
                gs[2 * s - 1].wait_recv()
            product(s, jnp.concatenate([pg[2 * s - 2], pg[2 * s - 1]], 0))
        st[s]["pair"] = copy(v.at[s, rows_of(theirs, half)], pair.at[s], other)

    def s1(s):
        st[s]["pair"].wait_recv()
        acc[s] = v[s, rows_of(mine, half), :] + pair[s]
        st[s]["m"] = [
            copy(acc.at[s, up(xf)], ring.at[s, 0], right), copy(acc.at[s, down(xf)], ring.at[s, 1], left),
            copy(acc.at[s, down(xa)], ring.at[s, 2], right), copy(acc.at[s, up(xb)], ring.at[s, 3], left),
        ]

    def s2(s):
        m = st[s]["m"]
        m[0].wait_recv()
        ring[s, 6] = acc[s, up(xa), :] + ring[s, 0]
        m.append(copy(ring.at[s, 6], ring.at[s, 4], right))
        m[1].wait_recv()
        ring[s, 7] = acc[s, down(xb), :] + ring[s, 1]
        m.append(copy(ring.at[s, 7], ring.at[s, 5], left))

    def s3(s):
        for m in st[s]["m"][2:]:
            m.wait_recv()
        acc[s, up(x), :] = acc[s, up(x), :] + (ring[s, 3] + ring[s, 4])
        acc[s, down(x), :] = acc[s, down(x), :] + (ring[s, 2] + ring[s, 5])
        st[s]["z"] = [copy(acc.at[(s,) + zpart(wz(z + d))], zb.at[s, d - 1], zs[d - 1]) for d in range(1, NZ)]

    def s4(s):
        for m in st[s]["z"]:
            m.wait_recv()
        r, l = zpart(z)
        t = acc[s, r, l]
        for d in range(NZ - 1):
            t = t + zb[s, d]
        t = t * scale
        zfin[s] = t
        r = rows_of(mine + x * pa + lax.div(z, 2) * zrow, zrow)
        st[s]["zz"] = [copy(zfin.at[s], fin.at[s, r, l], zs[d - 1]) for d in range(1, NZ)]
        fin[s, r, l] = t

    def s5(s):
        for m in st[s]["zz"]:
            m.wait_recv()
        f = lambda r: fin.at[s, r]
        fu = lambda q: f(rows_of(mine + q * pa, h))
        fd = lambda q: f(rows_of(mine + q * pa + h, h))
        st[s]["x"] = [
            copy(fu(x), fu(x), right), copy(fd(x), fd(x), left), copy(fd(x), fd(x), right), copy(fu(x), fu(x), left),
        ]
        whole = f(rows_of(mine + x * pa, pa))
        st[s]["o"] = [copy(whole, whole, other)]

    def s6(s):
        f = lambda r: fin.at[s, r]
        fu, fd = f(rows_of(mine + xb * pa, h)), f(rows_of(mine + xa * pa + h, h))
        m = st[s]["x"]
        m[0].wait_recv()
        m.append(copy(fu, fu, right))
        m[1].wait_recv()
        m.append(copy(fd, fd, left))

    def s7(s):
        m = st[s]["x"]
        m[2].wait_recv()
        m[3].wait_recv()
        for q in (xb, xa):
            whole = fin.at[s, rows_of(mine + q * pa, pa)]
            st[s]["o"].append(copy(whole, whole, other))
        m[4].wait_recv()
        m[5].wait_recv()
        whole = fin.at[s, rows_of(mine + xf * pa, pa)]
        st[s]["o"].append(copy(whole, whole, other))

    def s8(s):
        for m in st[s]["o"]:
            m.wait_recv()
        for i in range(2):
            to, frm = lanes_of(at[s][i], hp), pl.ds(i * hp, hp)
            block = fin[s, pl.ds(0, nq), frm]
            coeffs[:, to] = block
            ch[:, to], cl[:, to] = halves(block)
            pp[:, to] = fin[s, pl.ds(nq, npan), frm]

    rest = {}

    def s9(s):
        t = dot3(halves(fin[s, pl.ds(0, nq), :]), (wh[pl.ds(0, nq)], wl[pl.ds(0, nq)]), TN)
        s_ref[s] = t
        lo, hi = s_ref.at[s, pl.ds(0, hp)], s_ref.at[s, pl.ds(hp, hp)]
        if s == 1:
            rest["c"] = copy(hi, mid.at[2], north)
            rest["d"] = copy(lo, mid.at[3], south)
        if s == 3:
            rest["a"] = copy(lo, mid.at[0], north)
            rest["b"] = copy(hi, mid.at[1], south)

    ng = part.shape[0]
    gq = ng // NY

    def g0():
        for u, rb in enumerate((x, 7 - x)):
            ct[...] = coeffs[:, lanes_of(rb * 128, 128)].T
            rs[pl.ds(u * 64, 64), pl.ds(0, nq)] = ct[rows_of(c * 64, 64), :]
        prod = dot3(halves(rs[:, pl.ds(0, nq)]), (ch[...], cl[...]), NN)
        rs[...] = prod
        for k in range(9):
            first = k < 8 - x
            rb = jnp.where(first, x, 7 - x)
            cb = jnp.where(first, x + k, k - 1)
            u = jnp.where(first, 0, 1)
            l = lanes_of(cb * 128, 128)
            own = (lax.div(rb, 2) == y).astype(F32)
            part[:, pl.ds(k * 128, 128)] = own * pp[rows_of(lax.rem(rb, 2) * 128 + c * 64, 64), l] - rs[rows_of(u * 64, 64), l]
        rest["r1"] = [copy(part.at[rows_of(wy(y + d) * gq, gq)], yb.at[d - 1], ys[d - 1]) for d in (2, 1, 3)]

    gbase = c * (ng * NX)

    def g1():
        for m in rest["r1"]:
            m.wait_recv()
        t = part[rows_of(y * gq, gq)]
        for d in range(NY - 1):
            t = t + yb[d]
        gfin[...] = t
        to = rows_of(gbase + x * ng + y * gq, gq)
        rest["r2"] = [copy(gfin, g.at[to], ys[d - 1]) for d in (2, 1, 3)]
        g[to] = t

    def g2():
        for m in rest["r2"]:
            m.wait_recv()
        block = lambda b: g.at[rows_of(gbase + b * ng, ng)]
        last = []
        parts = ring_gather(copy, g, gbase, ng, x, right, left, wx, NX)
        got = next(parts)
        last.append(copy(block(x), block(x), other))
        last.append(copy(block(got), block(got), other))
        for got in parts:
            last.append(copy(block(got), block(got), other))
        rest["last"] = last

    def g3():
        rest["a"].wait_recv()
        mid[6] = mid[0] + s_ref[2, pl.ds(hp, hp), :]
        rest["e"] = copy(mid.at[6], mid.at[4], north)
        rest["b"].wait_recv()
        mid[7] = mid[1] + s_ref[2, pl.ds(0, hp), :]
        rest["f"] = copy(mid.at[7], mid.at[5], south)
        for m in rest["last"]:
            m.wait_recv()

    stages = (s0, s1, s2, s3, s4, s5, s6, s7, s8, s9)
    order = [(START[s] + AFTER[k], s, stages[k]) for s in range(4) for k in range(9)]
    order += [(START[s] + AFTER[8] + 0.1, s, s9) for s in range(3)]
    for _, s, stage in sorted(order, key=lambda e: e[:2]):
        stage(s)
    g0()
    s9(3)
    g1()
    g2()
    g3()
    first = lambda b: rows_of(b * npan, hp)
    second = lambda b: rows_of(b * npan + hp, hp)
    upper = lambda b: whole.at[first(b)]
    lower = lambda b: whole.at[second(b)]
    own = [
        plan(upper(y), upper(y), north), plan(lower(y), lower(y), south),
        plan(lower(y), lower(y), north), plan(upper(y), upper(y), south),
    ]
    pass_on = [plan(upper(yb_), upper(yb_), north), plan(lower(ya), lower(ya), south)]

    def scattered():
        rest["d"].wait_recv()
        rest["e"].wait_recv()
        whole[first(y)] = p_ref[pl.ds(0, hp)] - (s_ref[0, pl.ds(0, hp), :] + (mid[3] + mid[4]))
        own[0].start()
        rest["c"].wait_recv()
        rest["f"].wait_recv()
        whole[second(y)] = p_ref[pl.ds(hp, hp)] - (s_ref[0, pl.ds(hp, hp), :] + (mid[2] + mid[5]))
        for m in own[1:]:
            m.start()

    def passed():
        for i in range(2):
            own[i].wait_recv()
            pass_on[i].start()

    factorize(g, m_ref, th, tl, {SCATTERED_AT: scattered, PASSED_AT: passed})

    def share(b):
        return dot3(halves(m_ref[rows_of(y * npan, npan), lanes_of(b * npan, npan)]), halves(whole[rows_of(b * npan, npan), :]), NN)

    out[...] = share(y)
    own[2].wait_recv()
    out[...] = out[...] + share(yb_)
    own[3].wait_recv()
    out[...] = out[...] + share(ya)
    for m in pass_on:
        m.wait_recv()
    out[...] = out[...] + share(yf)
    for m in made:
        m.wait_send()


START = (3.0, 13.0, 24.5, 36.0)
AFTER = (0.0, 2.0, 5.0, 8.0, 15.0, 22.0, 25.0, 28.0, 30.0)


def step(basis, panel, scale):
    nq, w = basis.shape
    npan = panel.shape[0]
    total = npan * NY
    n = nq + npan
    half = n // 2
    pa = half // NX
    hp = npan // 2
    space = pl.BlockSpec(memory_space=pltpu.VMEM)
    short = [(n, w), (n, w), (nq, total), (nq, total), (B, total), (B, total)]
    shapes = [
        (6, hp, w), (4, n, 2 * hp), (4, half, 2 * hp), (4, half, 2 * hp), (4, 8, pa // 2, 2 * hp),
        (4, NZ - 1, pa * 2 // NZ, 128), (4, pa * 2 // NZ, 128), (4, n, 2 * hp),
        (npan, total), (128, nq), (128, total), (64, 9 * 128), (4, npan, w), (512, 9 * 128), (total, total),
        (NY - 1, 64 // NY, 9 * 128), (64 // NY, 9 * 128), (8, hp, w), (total, w),
    ]
    copies = 6 + 4 * (1 + 6 + 7 + 7 + 6 + 4) + 28
    return pl.pallas_call(
        functools.partial(step_kernel, scale),
        name="step",
        out_shape=[jax.ShapeDtypeStruct((npan, w), F32), jax.ShapeDtypeStruct((nq, total), F32)],
        in_specs=[space] * 2,
        out_specs=[space] * 2,
        scratch_shapes=[pltpu.VMEM(s_, BF16) for s_ in short] + [pltpu.VMEM(s_, F32) for s_ in shapes]
        + [pltpu.SemaphoreType.DMA((copies,)), pltpu.SemaphoreType.DMA((copies,))],
        compiler_params=pltpu.CompilerParams(collective_id=1, has_side_effects=True, vmem_limit_bytes=60 * 2**20),
    )(basis, panel)


def body(basis, panel):
    n_grid = panel.shape[1] * lax.axis_size("grid")
    return tuple(step(basis, panel, 1.0 / n_grid))


def solution(mesh):
    placed = (P("band", "grid"), P("band", "grid"))
    return jax.shard_map(
        body, mesh=mesh, in_specs=placed, out_specs=(P("band", "grid"), P("band", None)), check_vma=False,
    )
```

time: 492 us -> 173 us (0.35)
  waiting for transfers between devices: 380 us -> 0 us
  Pallas kernels: 41.5 us -> 168 us
  matrix products: 28.2 us -> 0 us
  between operations: 13.9 us -> 0.65 us
  other arithmetic: 11.1 us -> 0 us
  local copies, waits for them, and re-layouts: 11.4 us -> 3.78 us
  starting transfers between devices: 5.32 us -> 0 us
    psum x1 -> x0, waiting for transfers between devices: 192 us -> none  [together(): total = lax.psum(ravelled, axis)]
    pallas_call x1, Pallas kernels: 41.5 us -> 168 us  [step(): pl.pallas_call(functools.partial(step_kernel, scale), name='step', out_sh...]
    all_gather x3 -> x0, waiting for transfers between devices: 112 us -> none  [the longest x1 56.3 us: body(): both = tdot(stacked, lax.all_gather(panel, 'band', axis=0, tiled=True))]
    all_to_all x1 -> x0, waiting for transfers between devices: 75.7 us -> none  [summed_on_arrival(): lax.all_to_all(blocks, axis, split_axis=0, concat_axis=0, tiled=True)]
    dot_general x4 -> x0, matrix products: 28.2 us -> none  [the longest x3 19.8 us: ndot(): return jnp.dot(left, right, precision=lax.Precision.HIGH)]
    all_to_all x1 -> x0, starting transfers between devices: 4.93 us -> none  [summed_on_arrival(): lax.all_to_all(blocks, axis, split_axis=0, concat_axis=0, tiled=True)]
  transfers between devices with their start and end apart: 6 -> 0, of which waited for: 5 -> 0; matrix products, arithmetic and copies ran while one was open for 4% -> 0% of each run, Pallas kernels for 8% -> 0%
where the time goes in v4:
time: 173 us; the launch traced here: 172 us
  Pallas kernels  168 us (97%)
  local copies, waits for them, and re-layouts  3.78 us (2%)
    pallas_call x1, Pallas kernels, step(): pl.pallas_call(functools.partial(step_kernel, scale), name='step', out_sh...  168 us
    unnamed x4, local copies, waits for them, and re-layouts  3.78 us

profile of v4, /device:TPU:1, one launch (start us, length us, event | category | flops | bytes accessed | tf_op | source)
XLA Modules:
  0.0 172.4 jit_solution(14188535054396824652)
XLA Ops:
  0.6 168.0 %step.1 = (f32[256,1024]{1,0:T(8,128)}, f32[512,1024]{1,0:T(8,128)}) custom-call(f32[512,1024]{1,0:T(8,128)} %q_ref.1, f32[256,1024]{1,0:T(8,128)} %p_ref.1), custom_call_target="tpu_custom_call" | custom-call | tf_op jit(solution)/shard_map/step/pallas_call | solution.py:474
  168.6 0.0 copy-start
  168.7 2.5 %copy.6 = f32[256,1024]{1,0:T(8,128)} copy(f32[256,1024]{1,0:T(8,128)} %get-tuple-element.4) | data formatting | bytes 2097152
  171.1 0.0 copy-done
  171.1 1.3 copy.7
Async XLA Ops:
  168.6 2.5 %copy-start = (f32[512,1024]{1,0:T(8,128)S(1)}, f32[512,1024]{1,0:T(8,128)}, u32[]{:S(2)}) copy-start(f32[512,1024]{1,0:T(8,128)} %get-tuple-element.5) | copy-start | bytes 6291460

commit v5 on v4

--- a/solution.py
+++ b/solution.py
@@ -63,7 +63,7 @@
         end = at + BASE
         if end < n:
             parts = halves(v)
-            upd = lax.dot_general(v, v, (TN, ((), ())), precision=lax.Precision.HIGHEST, preferred_element_type=F32)
+            upd = dot3(parts, parts, TN)
             below = w[end:]
             l2 = lane[end:]
             below = jnp.where((l2 >= at) & (l2 < end), 0.0, below) - upd[end:]
@@ -75,11 +75,12 @@
 B = 128
 
 
-SCATTERED_AT, PASSED_AT = 0, 3
+SEGMENTS = ((0, 1, 0), (1, 4, 6), (4, 8, 3))
+SPARE = 4
 
 
 def factorize(g_ref, m_ref, th, tl, between):
-    n = m_ref.shape[0]
+    n = m_ref.shape[1]
     nb = n // B
     hb = g_ref.shape[0] // 2
     for t in range(nb // 2):
@@ -88,30 +89,33 @@
             m_ref[pl.ds(t * B + c * 64, 64), pl.ds(t * B, n - t * B)] = g_ref[src, pl.ds(0, n - t * B)]
             u = nb - 1 - t
             m_ref[pl.ds(u * B + c * 64, 64), pl.ds(u * B, n - u * B)] = g_ref[src, pl.ds(n - t * B, n - u * B)]
-
-    def step(k, _):
-        r = pl.multiple_of(k * B, B)
-        inv = factor128(m_ref[pl.ds(r, B), pl.ds(r, B)])
-        t = dot3(halves(inv), halves(m_ref[pl.ds(r, B), :]), NN)
-        m_ref[pl.ds(r, B), :] = t
-        m_ref[pl.ds(r, B), pl.ds(r, B)] = inv
-        hi, lo = halves(m_ref[pl.ds(r, B), :])
-        th[...] = hi
-        tl[...] = lo
-
-        def rest(i, _):
-            q = pl.multiple_of(i * B, B)
-            m_ref[pl.ds(q, B), pl.ds(r, B)] = jnp.zeros((B, B), F32)
-            f = (th[:, pl.ds(q, B)], tl[:, pl.ds(q, B)])
-            m_ref[pl.ds(q, B), :] = m_ref[pl.ds(q, B), :] - dot3(f, (th[...], tl[...]), TN)
-            return 0
-        lax.fori_loop(k + 1, nb, rest, 0)
-        for when, act in between.items():
+    th[:, pl.ds(n, SPARE * B)] = jnp.zeros((B, SPARE * B), BF16)
+    tl[:, pl.ds(n, SPARE * B)] = jnp.zeros((B, SPARE * B), BF16)
+    block = lambda i, count=1: pl.ds(pl.multiple_of(i * B, B), count * B)
+
+    def update(i, count, k):
+        q = block(i, count)
+        m_ref[q, block(k)] = jnp.zeros((count * B, B), F32)
+        m_ref[q, :] = m_ref[q, :] - dot3((th[:, q], tl[:, q]), (th[:, :n], tl[:, :n]), TN)
+
+    def step(acts, count, k, _):
+        inv = factor128(m_ref[block(k), block(k)])
+        if count:
+            update(k + 1, count, k - 1)
+        t = dot3(halves(inv), halves(m_ref[block(k), :]), NN)
+        m_ref[block(k), :] = t
+        m_ref[block(k), block(k)] = inv
+        hi, lo = halves(m_ref[block(k), :])
+        th[:, :n] = hi
+        tl[:, :n] = lo
+        update(k + 1, 1, k)
+        for when, act in acts.items():
             pl.when(k == when)(act)
         return 0
-    lax.fori_loop(0, nb, step, 0)
-    for t in range(nb - 1):
-        m_ref[pl.ds(t * B, B), pl.ds(t * B + B, n - t * B - B)] = jnp.zeros((B, n - t * B - B), F32)
+
+    for a, z, count in SEGMENTS:
+        acts = {k: act for k, act in between.items() if a <= k < z}
+        lax.fori_loop(a, z, functools.partial(step, acts, count), 0)
 
 
 MESH = pl.DeviceIdType.MESH
@@ -163,30 +167,8 @@
     return pl.ds(pl.multiple_of(start, 128), count)
 
 
-def ring_gather(copy, out, base, count, mine, right, left, wrap, size):
-    half = count // 2
-    first = lambda q: out.at[rows_of(base + q * count, half)]
-    second = lambda q: out.at[rows_of(base + q * count + half, half)]
-    a = copy(first(mine), first(mine), right)
-    b = copy(second(mine), second(mine), left)
-    c = copy(second(mine), second(mine), right)
-    d = copy(first(mine), first(mine), left)
-    before, after, far = wrap(mine + size - 1), wrap(mine + 1), wrap(mine + 2)
-    a.wait_recv()
-    e = copy(first(before), first(before), right)
-    b.wait_recv()
-    f = copy(second(after), second(after), left)
-    c.wait_recv()
-    yield before
-    d.wait_recv()
-    yield after
-    e.wait_recv()
-    f.wait_recv()
-    yield far
-
-
 def step_kernel(
-    scale, q_ref, p_ref, out, coeffs, wh, wl, ch, cl, th, tl, pg, v, pair, acc, ring, zb, zfin, fin,
+    scale, q_ref, p_ref, out, coeffs, wh, wl, ch, cl, th, tl, rh, rl, pg, v, pair, acc, ring, zb, zfin, fin,
     pp, ct, rs, part, s_ref, g, m_ref, yb, gfin, mid, whole, send, recv,
 ):
     c, x, z, y = place()
@@ -331,6 +313,21 @@
 
     rest = {}
 
+    hq = hp // 2
+    part_of = lambda i: pl.ds(i * hq, hq)
+
+    def far_sum(i):
+        rest["a", i] = copy(s_ref.at[3, part_of(i)], mid.at[0, part_of(i)], north)
+        rest["b", i] = copy(s_ref.at[3, part_of(2 + i)], mid.at[1, part_of(i)], south)
+
+    def near_sum(i):
+        rest["a", i].wait_recv()
+        mid[6, part_of(i)] = mid[0, part_of(i)] + s_ref[2, part_of(2 + i), :]
+        rest["e", i] = copy(mid.at[6, part_of(i)], mid.at[4, part_of(i)], north)
+        rest["b", i].wait_recv()
+        mid[7, part_of(i)] = mid[1, part_of(i)] + s_ref[2, part_of(i), :]
+        rest["f", i] = copy(mid.at[7, part_of(i)], mid.at[5, part_of(i)], south)
+
     def s9(s):
         t = dot3(halves(fin[s, pl.ds(0, nq), :]), (wh[pl.ds(0, nq)], wl[pl.ds(0, nq)]), TN)
         s_ref[s] = t
@@ -339,8 +336,7 @@
             rest["c"] = copy(hi, mid.at[2], north)
             rest["d"] = copy(lo, mid.at[3], south)
         if s == 3:
-            rest["a"] = copy(lo, mid.at[0], north)
-            rest["b"] = copy(hi, mid.at[1], south)
+            far_sum(0)
 
     ng = part.shape[0]
     gq = ng // NY
@@ -372,30 +368,36 @@
         gfin[...] = t
         to = rows_of(gbase + x * ng + y * gq, gq)
         rest["r2"] = [copy(gfin, g.at[to], ys[d - 1]) for d in (2, 1, 3)]
+        far_sum(1)
         g[to] = t
 
     def g2():
         for m in rest["r2"]:
             m.wait_recv()
-        block = lambda b: g.at[rows_of(gbase + b * ng, ng)]
-        last = []
-        parts = ring_gather(copy, g, gbase, ng, x, right, left, wx, NX)
-        got = next(parts)
-        last.append(copy(block(x), block(x), other))
-        last.append(copy(block(got), block(got), other))
-        for got in parts:
-            last.append(copy(block(got), block(got), other))
-        rest["last"] = last
-
-    def g3():
-        rest["a"].wait_recv()
-        mid[6] = mid[0] + s_ref[2, pl.ds(hp, hp), :]
-        rest["e"] = copy(mid.at[6], mid.at[4], north)
-        rest["b"].wait_recv()
-        mid[7] = mid[1] + s_ref[2, pl.ds(0, hp), :]
-        rest["f"] = copy(mid.at[7], mid.at[5], south)
-        for m in rest["last"]:
-            m.wait_recv()
+        hg = ng // 2
+        upper = lambda b: g.at[rows_of(gbase + b * ng, hg)]
+        lower = lambda b: g.at[rows_of(gbase + b * ng + hg, hg)]
+        whole_of = lambda b: g.at[rows_of(gbase + b * ng, ng)]
+        m = [
+            copy(upper(x), upper(x), right), copy(lower(x), lower(x), left),
+            copy(lower(x), lower(x), right), copy(upper(x), upper(x), left),
+        ]
+        last = [copy(whole_of(x), whole_of(x), other)]
+        near_sum(0)
+        m[0].wait_recv()
+        m.append(copy(upper(xb), upper(xb), right))
+        m[1].wait_recv()
+        m.append(copy(lower(xa), lower(xa), left))
+        m[2].wait_recv()
+        last.append(copy(whole_of(xb), whole_of(xb), other))
+        m[3].wait_recv()
+        last.append(copy(whole_of(xa), whole_of(xa), other))
+        near_sum(1)
+        m[4].wait_recv()
+        m[5].wait_recv()
+        last.append(copy(whole_of(xf), whole_of(xf), other))
+        for q in last:
+            q.wait_recv()
 
     stages = (s0, s1, s2, s3, s4, s5, s6, s7, s8, s9)
     order = [(START[s] + AFTER[k], s, stages[k]) for s in range(4) for k in range(9)]
@@ -406,50 +408,70 @@
     s9(3)
     g1()
     g2()
-    g3()
-    first = lambda b: rows_of(b * npan, hp)
-    second = lambda b: rows_of(b * npan + hp, hp)
-    upper = lambda b: whole.at[first(b)]
-    lower = lambda b: whole.at[second(b)]
-    own = [
-        plan(upper(y), upper(y), north), plan(lower(y), lower(y), south),
-        plan(lower(y), lower(y), north), plan(upper(y), upper(y), south),
-    ]
-    pass_on = [plan(upper(yb_), upper(yb_), north), plan(lower(ya), lower(ya), south)]
-
-    def scattered():
-        rest["d"].wait_recv()
-        rest["e"].wait_recv()
-        whole[first(y)] = p_ref[pl.ds(0, hp)] - (s_ref[0, pl.ds(0, hp), :] + (mid[3] + mid[4]))
-        own[0].start()
-        rest["c"].wait_recv()
-        rest["f"].wait_recv()
-        whole[second(y)] = p_ref[pl.ds(hp, hp)] - (s_ref[0, pl.ds(hp, hp), :] + (mid[2] + mid[5]))
-        for m in own[1:]:
-            m.start()
+    upper = lambda b, at=0, count=hp: whole.at[rows_of(b * npan + at, count)]
+    lower = lambda b, at=0, count=hp: whole.at[rows_of(b * npan + hp + at, count)]
+    same = lambda ref, to: plan(ref, ref, to)
+    early = [[same(upper(y, i * hq, hq), north), same(lower(y, i * hq, hq), south)] for i in range(2)]
+    later = [same(lower(y), north), same(upper(y), south)]
+    pass_on = [same(upper(yb_), north), same(lower(ya), south)]
+
+    def split(b):
+        r = rows_of(b * npan, npan)
+        rh[r, :], rl[r, :] = halves(whole[r, :])
+
+    def summed(i):
+        def act():
+            if i == 0:
+                rest["d"].wait_recv()
+                rest["c"].wait_recv()
+            p = part_of(i)
+            q = part_of(2 + i)
+            rest["e", i].wait_recv()
+            whole[rows_of(y * npan + i * hq, hq)] = p_ref[p] - (s_ref[0, p, :] + (mid[3, p] + mid[4, p]))
+            early[i][0].start()
+            rest["f", i].wait_recv()
+            whole[rows_of(y * npan + hp + i * hq, hq)] = p_ref[q] - (s_ref[0, q, :] + (mid[2, p] + mid[5, p]))
+            early[i][1].start()
+            if i == 1:
+                for m in later:
+                    m.start()
+        return act
 
     def passed():
         for i in range(2):
-            own[i].wait_recv()
+            early[0][i].wait_recv()
+            early[1][i].wait_recv()
             pass_on[i].start()
 
-    factorize(g, m_ref, th, tl, {SCATTERED_AT: scattered, PASSED_AT: passed})
-
-    def share(b):
-        return dot3(halves(m_ref[rows_of(y * npan, npan), lanes_of(b * npan, npan)]), halves(whole[rows_of(b * npan, npan), :]), NN)
-
-    out[...] = share(y)
-    own[2].wait_recv()
-    out[...] = out[...] + share(yb_)
-    own[3].wait_recv()
-    out[...] = out[...] + share(ya)
+    def near():
+        split(y)
+        for m in later:
+            m.wait_recv()
+        split(yb_)
+        split(ya)
+
+    factorize(g, m_ref, th, tl, dict(zip(HOOKS, (summed(0), summed(1), passed, near))))
+    mine_rows = m_ref[rows_of(y * npan, npan), :]
+    total = mine_rows.shape[1]
+    row = lax.broadcasted_iota(jnp.int32, (npan, total), 0) + y * npan
+    col = lax.broadcasted_iota(jnp.int32, (npan, total), 1)
+    xh, xl = halves(jnp.where(col <= row, mine_rows, 0.0))
+    ch[pl.ds(0, npan)], cl[pl.ds(0, npan)] = xh, xl
     for m in pass_on:
         m.wait_recv()
-    out[...] = out[...] + share(yf)
+    split(yf)
+
+    def columns(i, _):
+        l = lanes_of(i * 256, 256)
+        out[:, l] = dot3((ch[pl.ds(0, npan)], cl[pl.ds(0, npan)]), (rh[:, l], rl[:, l]), NN)
+        return 0
+
+    lax.fori_loop(0, out.shape[1] // 256, columns, 0)
     for m in made:
         m.wait_send()
 
 
+HOOKS = (0, 1, 3, 6)
 START = (3.0, 13.0, 24.5, 36.0)
 AFTER = (0.0, 2.0, 5.0, 8.0, 15.0, 22.0, 25.0, 28.0, 30.0)
 
@@ -463,14 +485,14 @@
     pa = half // NX
     hp = npan // 2
     space = pl.BlockSpec(memory_space=pltpu.VMEM)
-    short = [(n, w), (n, w), (nq, total), (nq, total), (B, total), (B, total)]
+    short = [(n, w), (n, w), (nq, total), (nq, total)] + [(B, total + SPARE * B)] * 2 + [(total, w)] * 2
     shapes = [
         (6, hp, w), (4, n, 2 * hp), (4, half, 2 * hp), (4, half, 2 * hp), (4, 8, pa // 2, 2 * hp),
         (4, NZ - 1, pa * 2 // NZ, 128), (4, pa * 2 // NZ, 128), (4, n, 2 * hp),
-        (npan, total), (128, nq), (128, total), (64, 9 * 128), (4, npan, w), (512, 9 * 128), (total, total),
+        (npan, total), (128, nq), (128, total), (64, 9 * 128), (4, npan, w), (512, 9 * 128), (total + SPARE * B, total),
         (NY - 1, 64 // NY, 9 * 128), (64 // NY, 9 * 128), (8, hp, w), (total, w),
     ]
-    copies = 6 + 4 * (1 + 6 + 7 + 7 + 6 + 4) + 28
+    copies = 6 + 4 * (1 + 6 + 7 + 7 + 6 + 4) + 34
     return pl.pallas_call(
         functools.partial(step_kernel, scale),
         name="step",

time: 173 us -> 162 us (0.936)
  Pallas kernels: 168 us -> 158 us
    pallas_call x1, Pallas kernels: 168 us -> 158 us  [step(): pl.pallas_call(functools.partial(step_kernel, scale), name='step', out_sh...]
where the time goes in v5:
time: 162 us
  Pallas kernels  158 us (98%)
  local copies, waits for them, and re-layouts  3.78 us (2%)
    pallas_call x1, Pallas kernels, step(): pl.pallas_call(functools.partial(step_kernel, scale), name='step', out_sh...  158 us
    unnamed x4, local copies, waits for them, and re-layouts  3.78 us

profile of v5, /device:TPU:1, one launch (start us, length us, event | category | flops | bytes accessed | tf_op | source)
XLA Modules:
  0.0 162.1 jit_solution(11750205990043823951)
XLA Ops:
  0.6 157.7 %step.1 = (f32[256,1024]{1,0:T(8,128)}, f32[512,1024]{1,0:T(8,128)}) custom-call(f32[512,1024]{1,0:T(8,128)} %q_ref.1, f32[256,1024]{1,0:T(8,128)} %p_ref.1), custom_call_target="tpu_custom_call" | custom-call | tf_op jit(solution)/shard_map/step/pallas_call | solution.py:496
  158.3 0.0 copy-start
  158.4 2.5 %copy.6 = f32[256,1024]{1,0:T(8,128)} copy(f32[256,1024]{1,0:T(8,128)} %get-tuple-element.4) | data formatting | bytes 2097152
  160.8 0.0 copy-done
  160.8 1.3 copy.7
Async XLA Ops:
  158.3 2.5 %copy-start = (f32[512,1024]{1,0:T(8,128)S(1)}, f32[512,1024]{1,0:T(8,128)}, u32[]{:S(2)}) copy-start(f32[512,1024]{1,0:T(8,128)} %get-tuple-element.5) | copy-start | bytes 6291460

commit v6 on v5

--- a/solution.py
+++ b/solution.py
@@ -168,8 +168,8 @@
 
 
 def step_kernel(
-    scale, q_ref, p_ref, out, coeffs, wh, wl, ch, cl, th, tl, rh, rl, pg, v, pair, acc, ring, zb, zfin, fin,
-    pp, ct, rs, part, s_ref, g, m_ref, yb, gfin, mid, whole, send, recv,
+    scale, q_ref, p_ref, out, coeffs_hbm, wh, wl, ch, cl, th, tl, rh, rl, pg, v, pair, acc, ring, zb, zfin, fin,
+    pp, ct, rs, part, s_ref, g, m_ref, yb, gfin, mid, whole, coeffs, send, recv, done,
 ):
     c, x, z, y = place()
     nq, npan = q_ref.shape[0], p_ref.shape[0]
@@ -190,10 +190,14 @@
     yb_, ya, yf = wy(y + NY - 1), wy(y + 1), wy(y + 2)
     hp = npan // 2
     p1, p2 = p_ref.at[pl.ds(0, hp)], p_ref.at[pl.ds(hp, hp)]
-    gs = [copy(p1, pg.at[0], north), copy(p2, pg.at[1], south), copy(p2, pg.at[2], north), copy(p1, pg.at[3], south)]
+    lead, tail = pl.ds(0, hp // 4), pl.ds(hp // 4, hp - hp // 4)
+    gs = [
+        copy(p1, pg.at[0], north), copy(p2, pg.at[1], south),
+        copy(p2.at[lead], pg.at[2, lead], north), copy(p1.at[lead], pg.at[3, lead], south),
+    ]
     at = [
         (y * npan, y * npan + hp), (yb_ * npan, ya * npan + hp),
-        (yb_ * npan + hp, ya * npan), (yf * npan, yf * npan + hp),
+        (yf * npan, yf * npan + hp), (yb_ * npan + hp, ya * npan),
     ]
     wh[pl.ds(0, nq)], wl[pl.ds(0, nq)] = halves(q_ref[...])
     wh[pl.ds(nq, npan)], wl[pl.ds(nq, npan)] = halves(p_ref[...])
@@ -223,12 +227,14 @@
             if s == 1:
                 gs[0].wait_recv()
                 gs.append(copy(pg.at[0], pg.at[4], north))
+                gs.append(copy(p2.at[tail], pg.at[2, tail], north))
                 gs[1].wait_recv()
                 gs.append(copy(pg.at[1], pg.at[5], south))
-            else:
-                gs[2 * s - 2].wait_recv()
-                gs[2 * s - 1].wait_recv()
-            product(s, jnp.concatenate([pg[2 * s - 2], pg[2 * s - 1]], 0))
+                gs.append(copy(p1.at[tail], pg.at[3, tail], south))
+            for m in {1: (), 2: (4, 6), 3: (2, 3, 5, 7)}[s]:
+                gs[m].wait_recv()
+            u = {1: 0, 2: 4, 3: 2}[s]
+            product(s, jnp.concatenate([pg[u], pg[u + 1]], 0))
         st[s]["pair"] = copy(v.at[s, rows_of(theirs, half)], pair.at[s], other)
 
     def s1(s):
@@ -313,20 +319,23 @@
 
     rest = {}
 
-    hq = hp // 2
-    part_of = lambda i: pl.ds(i * hq, hq)
+    hq = hp // 4
+    far_parts = {"a": [], "b": []}
 
     def far_sum(i):
-        rest["a", i] = copy(s_ref.at[3, part_of(i)], mid.at[0, part_of(i)], north)
-        rest["b", i] = copy(s_ref.at[3, part_of(2 + i)], mid.at[1, part_of(i)], south)
-
-    def near_sum(i):
-        rest["a", i].wait_recv()
-        mid[6, part_of(i)] = mid[0, part_of(i)] + s_ref[2, part_of(2 + i), :]
-        rest["e", i] = copy(mid.at[6, part_of(i)], mid.at[4, part_of(i)], north)
-        rest["b", i].wait_recv()
-        mid[7, part_of(i)] = mid[1, part_of(i)] + s_ref[2, part_of(i), :]
-        rest["f", i] = copy(mid.at[7, part_of(i)], mid.at[5, part_of(i)], south)
+        p = pl.ds(i * hq, hq)
+        far_parts["a"].append(copy(s_ref.at[2, p], mid.at[0, p], north))
+        far_parts["b"].append(copy(s_ref.at[2, pl.ds(hp + i * hq, hq)], mid.at[1, p], south))
+
+    def near_sum():
+        for m in far_parts["a"]:
+            m.wait_recv()
+        mid[6] = mid[0] + s_ref[3, pl.ds(hp, hp), :]
+        rest["e"] = copy(mid.at[6], mid.at[4], north)
+        for m in far_parts["b"]:
+            m.wait_recv()
+        mid[7] = mid[1] + s_ref[3, pl.ds(0, hp), :]
+        rest["f"] = copy(mid.at[7], mid.at[5], south)
 
     def s9(s):
         t = dot3(halves(fin[s, pl.ds(0, nq), :]), (wh[pl.ds(0, nq)], wl[pl.ds(0, nq)]), TN)
@@ -335,8 +344,9 @@
         if s == 1:
             rest["c"] = copy(hi, mid.at[2], north)
             rest["d"] = copy(lo, mid.at[3], south)
-        if s == 3:
+        if s == 2:
             far_sum(0)
+            far_sum(1)
 
     ng = part.shape[0]
     gq = ng // NY
@@ -356,6 +366,7 @@
             own = (lax.div(rb, 2) == y).astype(F32)
             part[:, pl.ds(k * 128, 128)] = own * pp[rows_of(lax.rem(rb, 2) * 128 + c * 64, 64), l] - rs[rows_of(u * 64, 64), l]
         rest["r1"] = [copy(part.at[rows_of(wy(y + d) * gq, gq)], yb.at[d - 1], ys[d - 1]) for d in (2, 1, 3)]
+        far_sum(3)
 
     gbase = c * (ng * NX)
 
@@ -368,8 +379,24 @@
         gfin[...] = t
         to = rows_of(gbase + x * ng + y * gq, gq)
         rest["r2"] = [copy(gfin, g.at[to], ys[d - 1]) for d in (2, 1, 3)]
-        far_sum(1)
         g[to] = t
+        near_sum()
+
+    def summed():
+        upper = lambda b: whole.at[rows_of(b * npan, hp)]
+        lower = lambda b: whole.at[rows_of(b * npan + hp, hp)]
+        same = lambda ref, to: plan(ref, ref, to)
+        rest["d"].wait_recv()
+        rest["e"].wait_recv()
+        whole[rows_of(y * npan, hp)] = p_ref[pl.ds(0, hp)] - (s_ref[0, pl.ds(0, hp), :] + (mid[3] + mid[4]))
+        early = [copy(upper(y), upper(y), north)]
+        rest["c"].wait_recv()
+        rest["f"].wait_recv()
+        whole[rows_of(y * npan + hp, hp)] = p_ref[pl.ds(hp, hp)] - (s_ref[0, pl.ds(hp, hp), :] + (mid[2] + mid[5]))
+        early.append(copy(lower(y), lower(y), south))
+        rest["early"] = early
+        rest["later"] = [copy(lower(y), lower(y), north), copy(upper(y), upper(y), south)]
+        rest["pass_on"] = [same(upper(yb_), north), same(lower(ya), south)]
 
     def g2():
         for m in rest["r2"]:
@@ -383,7 +410,6 @@
             copy(lower(x), lower(x), right), copy(upper(x), upper(x), left),
         ]
         last = [copy(whole_of(x), whole_of(x), other)]
-        near_sum(0)
         m[0].wait_recv()
         m.append(copy(upper(xb), upper(xb), right))
         m[1].wait_recv()
@@ -392,55 +418,38 @@
         last.append(copy(whole_of(xb), whole_of(xb), other))
         m[3].wait_recv()
         last.append(copy(whole_of(xa), whole_of(xa), other))
-        near_sum(1)
         m[4].wait_recv()
         m[5].wait_recv()
         last.append(copy(whole_of(xf), whole_of(xf), other))
+        summed()
         for q in last:
             q.wait_recv()
 
-    stages = (s0, s1, s2, s3, s4, s5, s6, s7, s8, s9)
+    def s6_far(s):
+        s6(s)
+        if s == 3:
+            far_sum(2)
+
+    stages = (s0, s1, s2, s3, s4, s5, s6_far, s7, s8, s9)
     order = [(START[s] + AFTER[k], s, stages[k]) for s in range(4) for k in range(9)]
     order += [(START[s] + AFTER[8] + 0.1, s, s9) for s in range(3)]
     for _, s, stage in sorted(order, key=lambda e: e[:2]):
         stage(s)
+    kept = pltpu.make_async_copy(coeffs, coeffs_hbm, done)
+    kept.start()
     g0()
     s9(3)
     g1()
     g2()
-    upper = lambda b, at=0, count=hp: whole.at[rows_of(b * npan + at, count)]
-    lower = lambda b, at=0, count=hp: whole.at[rows_of(b * npan + hp + at, count)]
-    same = lambda ref, to: plan(ref, ref, to)
-    early = [[same(upper(y, i * hq, hq), north), same(lower(y, i * hq, hq), south)] for i in range(2)]
-    later = [same(lower(y), north), same(upper(y), south)]
-    pass_on = [same(upper(yb_), north), same(lower(ya), south)]
-
     def split(b):
         r = rows_of(b * npan, npan)
         rh[r, :], rl[r, :] = halves(whole[r, :])
 
-    def summed(i):
-        def act():
-            if i == 0:
-                rest["d"].wait_recv()
-                rest["c"].wait_recv()
-            p = part_of(i)
-            q = part_of(2 + i)
-            rest["e", i].wait_recv()
-            whole[rows_of(y * npan + i * hq, hq)] = p_ref[p] - (s_ref[0, p, :] + (mid[3, p] + mid[4, p]))
-            early[i][0].start()
-            rest["f", i].wait_recv()
-            whole[rows_of(y * npan + hp + i * hq, hq)] = p_ref[q] - (s_ref[0, q, :] + (mid[2, p] + mid[5, p]))
-            early[i][1].start()
-            if i == 1:
-                for m in later:
-                    m.start()
-        return act
+    later, pass_on = rest["later"], rest["pass_on"]
 
     def passed():
         for i in range(2):
-            early[0][i].wait_recv()
-            early[1][i].wait_recv()
+            rest["early"][i].wait_recv()
             pass_on[i].start()
 
     def near():
@@ -450,7 +459,7 @@
         split(yb_)
         split(ya)
 
-    factorize(g, m_ref, th, tl, dict(zip(HOOKS, (summed(0), summed(1), passed, near))))
+    factorize(g, m_ref, th, tl, dict(zip(HOOKS, (passed, near))))
     mine_rows = m_ref[rows_of(y * npan, npan), :]
     total = mine_rows.shape[1]
     row = lax.broadcasted_iota(jnp.int32, (npan, total), 0) + y * npan
@@ -467,11 +476,12 @@
         return 0
 
     lax.fori_loop(0, out.shape[1] // 256, columns, 0)
+    kept.wait()
     for m in made:
         m.wait_send()
 
 
-HOOKS = (0, 1, 3, 6)
+HOOKS = (2, 5)
 START = (3.0, 13.0, 24.5, 36.0)
 AFTER = (0.0, 2.0, 5.0, 8.0, 15.0, 22.0, 25.0, 28.0, 30.0)
 
@@ -490,17 +500,17 @@
         (6, hp, w), (4, n, 2 * hp), (4, half, 2 * hp), (4, half, 2 * hp), (4, 8, pa // 2, 2 * hp),
         (4, NZ - 1, pa * 2 // NZ, 128), (4, pa * 2 // NZ, 128), (4, n, 2 * hp),
         (npan, total), (128, nq), (128, total), (64, 9 * 128), (4, npan, w), (512, 9 * 128), (total + SPARE * B, total),
-        (NY - 1, 64 // NY, 9 * 128), (64 // NY, 9 * 128), (8, hp, w), (total, w),
+        (NY - 1, 64 // NY, 9 * 128), (64 // NY, 9 * 128), (8, hp, w), (total, w), (nq, total),
     ]
-    copies = 6 + 4 * (1 + 6 + 7 + 7 + 6 + 4) + 34
+    copies = 6 + 4 * (1 + 6 + 7 + 7 + 6 + 4) + 36
     return pl.pallas_call(
         functools.partial(step_kernel, scale),
         name="step",
         out_shape=[jax.ShapeDtypeStruct((npan, w), F32), jax.ShapeDtypeStruct((nq, total), F32)],
         in_specs=[space] * 2,
-        out_specs=[space] * 2,
+        out_specs=[space, pl.BlockSpec(memory_space=pl.ANY)],
         scratch_shapes=[pltpu.VMEM(s_, BF16) for s_ in short] + [pltpu.VMEM(s_, F32) for s_ in shapes]
-        + [pltpu.SemaphoreType.DMA((copies,)), pltpu.SemaphoreType.DMA((copies,))],
+        + [pltpu.SemaphoreType.DMA((copies,)), pltpu.SemaphoreType.DMA((copies,)), pltpu.SemaphoreType.DMA(())],
         compiler_params=pltpu.CompilerParams(collective_id=1, has_side_effects=True, vmem_limit_bytes=60 * 2**20),
     )(basis, panel)
 

time: 162 us -> 160 us (0.988)
  Pallas kernels: 158 us -> 155 us
    pallas_call x1, Pallas kernels: 158 us -> 155 us  [step(): pl.pallas_call(functools.partial(step_kernel, scale), name='step', out_sh...]
where the time goes in v6:
time: 160 us; the launch traced here: 159 us
  Pallas kernels  155 us (97%)
  local copies, waits for them, and re-layouts  3.78 us (2%)
    pallas_call x1, Pallas kernels, step(): pl.pallas_call(functools.partial(step_kernel, scale), name='step', out_sh...  155 us
    unnamed x4, local copies, waits for them, and re-layouts  3.78 us

profile of v6, /device:TPU:1, one launch (start us, length us, event | category | flops | bytes accessed | tf_op | source)
XLA Modules:
  0.0 159.4 jit_solution(6898415338651306528)
XLA Ops:
  0.6 155.0 %step.1 = (f32[256,1024]{1,0:T(8,128)}, f32[512,1024]{1,0:T(8,128)}) custom-call(f32[512,1024]{1,0:T(8,128)} %q_ref.1, f32[256,1024]{1,0:T(8,128)} %p_ref.1), custom_call_target="tpu_custom_call" | custom-call | tf_op jit(solution)/shard_map/step/pallas_call | solution.py:506
  155.7 0.0 copy-start
  155.7 2.5 %copy.6 = f32[256,1024]{1,0:T(8,128)} copy(f32[256,1024]{1,0:T(8,128)} %get-tuple-element.4) | data formatting | bytes 2097152
  158.1 0.0 copy-done
  158.1 1.3 copy.7
Async XLA Ops:
  155.7 2.5 %copy-start = (f32[512,1024]{1,0:T(8,128)S(1)}, f32[512,1024]{1,0:T(8,128)}, u32[]{:S(2)}) copy-start(f32[512,1024]{1,0:T(8,128)} %get-tuple-element.5) | copy-start | bytes 6291460

commit v7 on v6

--- a/solution.py
+++ b/solution.py
@@ -432,13 +432,14 @@
 
     stages = (s0, s1, s2, s3, s4, s5, s6_far, s7, s8, s9)
     order = [(START[s] + AFTER[k], s, stages[k]) for s in range(4) for k in range(9)]
-    order += [(START[s] + AFTER[8] + 0.1, s, s9) for s in range(3)]
+    order += [(START[s] + AFTER[8] + 0.1, s, s9) for s in (1, 2)]
     for _, s, stage in sorted(order, key=lambda e: e[:2]):
         stage(s)
     kept = pltpu.make_async_copy(coeffs, coeffs_hbm, done)
     kept.start()
     g0()
     s9(3)
+    s9(0)
     g1()
     g2()
     def split(b):
@@ -482,8 +483,8 @@
 
 
 HOOKS = (2, 5)
-START = (3.0, 13.0, 24.5, 36.0)
-AFTER = (0.0, 2.0, 5.0, 8.0, 15.0, 22.0, 25.0, 28.0, 30.0)
+START = (3.0, 13.0, 27.0, 34.5)
+AFTER = (0.0, 2.0, 5.0, 8.0, 15.0, 22.0, 25.0, 28.0, 32.0)
 
 
 def step(basis, panel, scale):

time: 160 us -> 156 us (0.975)
  Pallas kernels: 155 us -> 151 us
    pallas_call x1, Pallas kernels: 155 us -> 151 us  [step(): pl.pallas_call(functools.partial(step_kernel, scale), name='step', out_sh...]
where the time goes in v7:
time: 156 us
  Pallas kernels  151 us (97%)
  local copies, waits for them, and re-layouts  3.78 us (2%)
    pallas_call x1, Pallas kernels, step(): pl.pallas_call(functools.partial(step_kernel, scale), name='step', out_sh...  151 us
    unnamed x4, local copies, waits for them, and re-layouts  3.78 us

profile of v7, /device:TPU:1, one launch (start us, length us, event | category | flops | bytes accessed | tf_op | source)
XLA Modules:
  0.0 155.6 jit_solution(10414211030734080665)
XLA Ops:
  0.6 151.2 %step.1 = (f32[256,1024]{1,0:T(8,128)}, f32[512,1024]{1,0:T(8,128)}) custom-call(f32[512,1024]{1,0:T(8,128)} %q_ref.1, f32[256,1024]{1,0:T(8,128)} %p_ref.1), custom_call_target="tpu_custom_call" | custom-call | tf_op jit(solution)/shard_map/step/pallas_call | solution.py:507
  151.8 0.0 copy-start
  151.8 2.5 %copy.6 = f32[256,1024]{1,0:T(8,128)} copy(f32[256,1024]{1,0:T(8,128)} %get-tuple-element.4) | data formatting | bytes 2097152
  154.3 0.0 copy-done
  154.3 1.3 copy.7
Async XLA Ops:
  151.8 2.5 %copy-start = (f32[512,1024]{1,0:T(8,128)S(1)}, f32[512,1024]{1,0:T(8,128)}, u32[]{:S(2)}) copy-start(f32[512,1024]{1,0:T(8,128)} %get-tuple-element.5) | copy-start | bytes 6291460

commit v8 on v7

--- a/solution.py
+++ b/solution.py
@@ -345,8 +345,8 @@
             rest["c"] = copy(hi, mid.at[2], north)
             rest["d"] = copy(lo, mid.at[3], south)
         if s == 2:
-            far_sum(0)
-            far_sum(1)
+            for i in range(3):
+                far_sum(i)
 
     ng = part.shape[0]
     gq = ng // NY
@@ -425,12 +425,7 @@
         for q in last:
             q.wait_recv()
 
-    def s6_far(s):
-        s6(s)
-        if s == 3:
-            far_sum(2)
-
-    stages = (s0, s1, s2, s3, s4, s5, s6_far, s7, s8, s9)
+    stages = (s0, s1, s2, s3, s4, s5, s6, s7, s8, s9)
     order = [(START[s] + AFTER[k], s, stages[k]) for s in range(4) for k in range(9)]
     order += [(START[s] + AFTER[8] + 0.1, s, s9) for s in (1, 2)]
     for _, s, stage in sorted(order, key=lambda e: e[:2]):

time: 156 us -> 156 us (level)
  no operation moved by 1% of the time
where the time goes in v8:
time: 156 us
  Pallas kernels  151 us (97%)
  local copies, waits for them, and re-layouts  3.78 us (2%)
    pallas_call x1, Pallas kernels, step(): pl.pallas_call(functools.partial(step_kernel, scale), name='step', out_sh...  151 us
    unnamed x4, local copies, waits for them, and re-layouts  3.78 us

profile of v8, /device:TPU:1, one launch (start us, length us, event | category | flops | bytes accessed | tf_op | source)
XLA Modules:
  0.0 155.6 jit_solution(8592309880059763935)
XLA Ops:
  0.6 151.2 %step.1 = (f32[256,1024]{1,0:T(8,128)}, f32[512,1024]{1,0:T(8,128)}) custom-call(f32[512,1024]{1,0:T(8,128)} %q_ref.1, f32[256,1024]{1,0:T(8,128)} %p_ref.1), custom_call_target="tpu_custom_call" | custom-call | tf_op jit(solution)/shard_map/step/pallas_call | solution.py:502
  151.8 0.0 copy-start
  151.8 2.5 %copy.6 = f32[256,1024]{1,0:T(8,128)} copy(f32[256,1024]{1,0:T(8,128)} %get-tuple-element.4) | data formatting | bytes 2097152
  154.3 0.0 copy-done
  154.3 1.3 copy.7
Async XLA Ops:
  151.8 2.5 %copy-start = (f32[512,1024]{1,0:T(8,128)S(1)}, f32[512,1024]{1,0:T(8,128)}, u32[]{:S(2)}) copy-start(f32[512,1024]{1,0:T(8,128)} %get-tuple-element.5) | copy-start | bytes 6291460
